TPU v7x, 8 devices: a whole 2x2x1 slice. The times are simulated.
8 devices in a mesh: dp: 8 (over z, y, x, core).
Axes of the slice: x: 2, y: 2, z: 1, core: 2. Of those that a mesh axis runs over, the one named last changes fastest.
Arguments:
- feats: bfloat16 [4096, 768], P('dp')
- frontier: int32 [262144], P('dp')
- nbr_l1: int32 [65536, 15], P('dp')
- mask_l1: int32 [65536, 15], P('dp')
- nbr_l2: int32 [16384, 10], P('dp')
- mask_l2: int32 [16384, 10], P('dp')
- nbr_l3: int32 [4096, 5], P('dp')
- mask_l3: int32 [4096, 5], P('dp')
- labels: int32 [4096], P('dp')
- seed_mask: int32 [4096], P('dp')
- params: float32 [604313], replicated
- adam_m: float32 [604313], replicated
- adam_v: float32 [604313], replicated
Outputs:
- output 1: float32 [], replicated
- output 2: float32 [604313], replicated
- output 3: float32 [604313], replicated
- output 4: float32 [604313], replicated
All inputs are finite; a program needn't handle non-finite values.
Results may differ from a plain program's by a relative error of at most 0.00173952.
Values are sent between devices in bfloat16 or wider.
A program may use at most 1 GiB of HBM per device.

v0:
```python
import jax
import jax.numpy as jnp
from jax import lax
from jax.sharding import PartitionSpec as P

HIDDEN = 256
STEP = 10
LN_EPS = 1e-5
BETA_ONE = 0.9
BETA_TWO = 0.999
ADAM_LR = 3e-3
ADAM_EPS = 1e-8


def param_shapes(feat, classes):
    return [(feat, HIDDEN), (feat, HIDDEN), (HIDDEN,), (HIDDEN,), (HIDDEN,),
            (HIDDEN, HIDDEN), (HIDDEN, HIDDEN), (HIDDEN,), (HIDDEN,), (HIDDEN,),
            (HIDDEN, classes), (HIDDEN, classes), (classes,)]


def class_count(n_params, feat):
    return (n_params - 2 * feat * HIDDEN - 6 * HIDDEN - 2 * HIDDEN * HIDDEN) // (2 * HIDDEN + 1)


def unpack(flat, feat, classes):
    pieces = []
    offset = 0
    for pshape in param_shapes(feat, classes):
        count_el = 1
        for extent in pshape:
            count_el = count_el * extent
        pieces.append(flat[offset:offset + count_el].reshape(pshape))
        offset = offset + count_el
    return pieces


def layer_post(z, gain, shift):
    act = jax.nn.relu(z)
    mean_act = jnp.mean(act, axis=-1, keepdims=True)
    centred = act - mean_act
    var_act = jnp.mean(centred * centred, axis=-1, keepdims=True)
    return centred * lax.rsqrt(var_act + LN_EPS) * gain + shift


def fetch_rows(local_table, ids, groups, cap):
    rows_dev = local_table.shape[0]
    n_req = ids.shape[0]
    owner = ids // rows_dev
    local_row = ids - owner * rows_dev
    order = jnp.argsort(owner, stable=True)
    sorted_owner = owner[order]
    counts = jax.ops.segment_sum(jnp.ones_like(owner), owner, num_segments=groups)
    starts = jnp.cumsum(counts) - counts
    slot = sorted_owner * cap + jnp.arange(n_req, dtype=jnp.int32) - starts[sorted_owner]
    request = jnp.zeros((groups * cap,), jnp.int32).at[slot].set(local_row[order])
    incoming = lax.all_to_all(request.reshape(groups, cap), 'dp', 0, 0)
    served = jnp.take(local_table, incoming.reshape(-1), axis=0).reshape(groups, cap, local_table.shape[1])
    returned = lax.all_to_all(served, 'dp', 0, 0)
    place = jnp.zeros((n_req,), jnp.int32).at[order].set(slot)
    return jnp.take(returned.reshape(groups * cap, local_table.shape[1]), place, axis=0)


def neighbor_mean(table, nbr_idx, nbr_mask):
    gathered = jnp.take(table, nbr_idx, axis=0)
    summed = jnp.einsum('nk,nkd->nd', nbr_mask.astype(jnp.bfloat16), gathered, preferred_element_type=jnp.float32)
    count = jnp.maximum(jnp.sum(nbr_mask, axis=-1).astype(jnp.float32), 1.0)
    return summed / count[:, None], count


def spread_back(grad_mean, nbr_idx, nbr_mask, count, out_rows):
    coef = nbr_mask.astype(jnp.float32) / count[:, None]
    contrib = coef[:, :, None] * grad_mean[:, None, :]
    return jax.ops.segment_sum(contrib.reshape(-1, grad_mean.shape[1]), nbr_idx.reshape(-1), num_segments=out_rows)


def add_prefix(full, head):
    head_rows = head.shape[0]
    return jnp.concatenate([full[:head_rows] + head, full[head_rows:]], axis=0)


def dense_pair(self_rows, agg_rows, w_self, w_nbr, bias):
    return (jnp.dot(self_rows, w_self, preferred_element_type=jnp.float32)
            + jnp.dot(agg_rows, w_nbr, preferred_element_type=jnp.float32) + bias)


def weight_grads(self_rows, agg_rows, d_outb, d_out):
    grad_self = jnp.einsum('nd,ne->de', self_rows, d_outb, preferred_element_type=jnp.float32)
    grad_nbr = jnp.einsum('nd,ne->de', agg_rows, d_outb, preferred_element_type=jnp.float32)
    return grad_self, grad_nbr, jnp.sum(d_out, axis=0)


def input_grads(d_outb, w_self, w_nbr):
    d_self = jnp.einsum('ne,de->nd', d_outb, w_self, preferred_element_type=jnp.float32)
    d_agg = jnp.einsum('ne,de->nd', d_outb, w_nbr, preferred_element_type=jnp.float32)
    return d_self, d_agg


def local_step(h_zero, nbr_l1, mask_l1, nbr_l2, mask_l2, nbr_l3, mask_l3, labels, seed_mask, pieces):
    weights_bf = [piece.astype(jnp.bfloat16) for piece in pieces]
    n_one = nbr_l1.shape[0]
    n_two = nbr_l2.shape[0]
    n_seed = labels.shape[0]
    classes = pieces[12].shape[0]
    agg_one, cnt_one = neighbor_mean(h_zero, nbr_l1, mask_l1)
    agg_one = agg_one.astype(jnp.bfloat16)
    self_one = h_zero[:n_one]
    z_one = dense_pair(self_one, agg_one, weights_bf[0], weights_bf[1], pieces[2])
    h_one, post_one = jax.vjp(layer_post, z_one, pieces[3], pieces[4])
    h_one = h_one.astype(jnp.bfloat16)
    agg_two, cnt_two = neighbor_mean(h_one, nbr_l2, mask_l2)
    agg_two = agg_two.astype(jnp.bfloat16)
    self_two = h_one[:n_two]
    z_two = dense_pair(self_two, agg_two, weights_bf[5], weights_bf[6], pieces[7])
    h_two, post_two = jax.vjp(layer_post, z_two, pieces[8], pieces[9])
    h_two = h_two.astype(jnp.bfloat16)
    agg_three, cnt_three = neighbor_mean(h_two, nbr_l3, mask_l3)
    agg_three = agg_three.astype(jnp.bfloat16)
    self_three = h_two[:n_seed]
    logits = dense_pair(self_three, agg_three, weights_bf[10], weights_bf[11], pieces[12])
    valid = seed_mask.astype(jnp.float32)
    total = jnp.maximum(lax.psum(jnp.sum(valid), 'dp'), 1.0)
    log_norm = jax.nn.logsumexp(logits, axis=-1)
    onehot = (labels[:, None] == jnp.arange(classes)[None, :]).astype(jnp.float32)
    picked = jnp.sum(logits * onehot, axis=-1)
    loss = lax.psum(jnp.sum((log_norm - picked) * valid), 'dp') / total
    d_logits = (jnp.exp(logits - log_norm[:, None]) - onehot) * (valid / total)[:, None]
    d_logb = d_logits.astype(jnp.bfloat16)
    grad_self3, grad_nbr3, grad_bias3 = weight_grads(self_three, agg_three, d_logb, d_logits)
    d_self3, d_agg3 = input_grads(d_logb, weights_bf[10], weights_bf[11])
    d_htwo = add_prefix(spread_back(d_agg3, nbr_l3, mask_l3, cnt_three, n_two), d_self3)
    d_ztwo, grad_gain2, grad_shift2 = post_two(d_htwo)
    d_ztwob = d_ztwo.astype(jnp.bfloat16)
    grad_self2, grad_nbr2, grad_bias2 = weight_grads(self_two, agg_two, d_ztwob, d_ztwo)
    d_self2, d_agg2 = input_grads(d_ztwob, weights_bf[5], weights_bf[6])
    d_hone = add_prefix(spread_back(d_agg2, nbr_l2, mask_l2, cnt_two, n_one), d_self2)
    d_zone, grad_gain1, grad_shift1 = post_one(d_hone)
    grad_self1, grad_nbr1, grad_bias1 = weight_grads(self_one, agg_one, d_zone.astype(jnp.bfloat16), d_zone)
    grads = jnp.concatenate([grad_self1.reshape(-1), grad_nbr1.reshape(-1), grad_bias1, grad_gain1, grad_shift1,
                             grad_self2.reshape(-1), grad_nbr2.reshape(-1), grad_bias2, grad_gain2, grad_shift2,
                             grad_self3.reshape(-1), grad_nbr3.reshape(-1), grad_bias3])
    return loss, grads


def adam_update(params, adam_m, adam_v, grads):
    m_new = BETA_ONE * adam_m + (1.0 - BETA_ONE) * grads
    v_new = BETA_TWO * adam_v + (1.0 - BETA_TWO) * grads * grads
    m_hat = m_new / (1.0 - BETA_ONE ** STEP)
    v_hat = v_new / (1.0 - BETA_TWO ** STEP)
    return (params - ADAM_LR * m_hat / (jnp.sqrt(v_hat) + ADAM_EPS), m_new, v_new)


def solution(mesh):
    groups = mesh.shape['dp']

    def body(feats, frontier, nbr_l1, mask_l1, nbr_l2, mask_l2, nbr_l3, mask_l3, labels, seed_mask, params, adam_m, adam_v):
        feat = feats.shape[1]
        classes = class_count(params.shape[0], feat)
        cap = (11 * frontier.shape[0]) // (4 * groups)
        h_zero = fetch_rows(feats, frontier, groups, cap)
        loss, grads = local_step(h_zero, nbr_l1, mask_l1, nbr_l2, mask_l2, nbr_l3, mask_l3, labels, seed_mask,
                                 unpack(params, feat, classes))
        grads = lax.psum(grads, 'dp')
        return (loss,) + adam_update(params, adam_m, adam_v, grads)

    row_spec = P('dp')
    replicated = P()
    return jax.shard_map(body, mesh=mesh, in_specs=(row_spec,) * 10 + (replicated,) * 3,
                         out_specs=(replicated,) * 4, check_vma=False)
```

profile of v0, /device:TPU:0, one launch (start us, length us, event | category | flops | bytes accessed | tf_op | source)
XLA Modules:
  0.0 6472.6 jit_solution(8086957752850451308)
XLA Ops:
  8.3 226.3 %scatter_custom_fusion = s32[8]{0:T(128)S(1)} fusion(s32[32768]{0:T(1024)S(1)} %get-tuple-element.43, s32[32768]{0:T(1024)S(1)} %ne.14, s32[]{:T(128)} %constant.69.clone.1), kind=kCustom, calls=%fused_computation.173 | custom fusion | flops 32768 | bytes 36 | tf_op jit(solution)/shard_map/scatter-add | solution.py:52
  235.5 11.2 sort.17
  247.3 192.1 %gather_fusion = s32[32768]{0:T(1024)S(1)} fusion(s32[32768]{0:T(1024)S(1)} %get-tuple-element.43, s32[32768]{0:T(1024)S(1)} %get-tuple-element.41), kind=kCustom, calls=%fused_computation | custom fusion | bytes 393216 | tf_op jit(solution)/shard_map/gather | solution.py:51
  439.9 4.9 compare_select_fusion.5
  446.4 180.5 %gather_fusion.1 = s32[32768]{0:T(1024)S(1)} fusion(s32[32768]{0:T(1024)S(1)} %get-tuple-element.42, s32[32768]{0:T(1024)S(1)} %get-tuple-element.41), kind=kCustom, calls=%fused_computation.1 | custom fusion | bytes 393216 | tf_op jit(solution)/shard_map/gather | solution.py:55
  627.0 120.2 %scatter_custom_fusion.2 = s32[90112]{0:T(1024)S(1)} fusion(s32[32768]{0:T(1024)S(1)} %bitcast.100, s32[32768]{0:T(1024)S(1)} %gather_fusion.1, s32[]{:T(128)} %constant.69.clone.1), kind=kCustom, calls=%fused_computation.119 | custom fusion | bytes 360452 | tf_op jit(solution)/shard_map/scatter | solution.py:55
  747.2 12.1 all_to_all.14
  760.4 369.0 %gather_fusion.2 = bf16[90112,768]{1,0:T(8,128)(2,1)} fusion(bf16[512,768]{1,0:T(8,128)(2,1)S(1)} %copy-done, s32[90112]{0:T(1024)S(1)} %broadcast_clamp_fusion.1), kind=kCustom, calls=%fused_computation.2 | custom fusion | bytes 277184512 | tf_op jit(solution)/shard_map/jit(_take)/gather | solution.py:57
  1129.6 90.4 %broadcast_select_fusion = bf16[8,11264,768]{2,1,0:T(8,128)(2,1)} fusion(bf16[8,11264,768]{2,1,0:T(8,128)(2,1)} %bitcast.17, pred[8,11264]{1,0:T(8,128)(4,1)S(1)} %compare_and_fusion.1), kind=kLoop, calls=%fused_computation.15 | loop fusion | flops 69206016 | bytes 276914176 | tf_op jit(solution)/shard_map/jit(_take)/select_n | solution.py:57
  1220.0 12.1 all-to-all-start.1
  1232.9 1504.8 %psum.22 = f32[]{:T(128)} all-reduce(f32[]{:T(128)} %convert_reduce_fusion), channel_id=1, replica_groups=mesh['dp'=8] {'dp'}, use_global_device_ids=true, to_apply=%region_18.19 | all-reduce | flops 1 | bytes 8 | tf_op jit(solution)/shard_map/psum | solution.py:121
  2739.9 2.7 copy.49
  2742.6 5.7 reshape.348
  2749.0 6.7 copy.70
  2755.9 2.2 copy.48
  2763.8 2.0 reshape.356
  2766.4 2.0 copy.72
  2781.2 2.6 mul.235
  2783.8 2.6 reshape.404
  2786.4 120.2 %scatter_custom_fusion.1 = s32[32768]{0:T(1024)S(1)} fusion(s32[32768]{0:T(1024)} %get-tuple-element.40, s32[32768]{0:T(1024)} %get-tuple-element.15, s32[]{:T(128)} %constant.69.clone.1), kind=kCustom, calls=%fused_computation.133 | custom fusion | bytes 131584 | tf_op jit(solution)/shard_map/scatter | solution.py:59
  2910.6 564.8 %gather_fusion.3 = bf16[32768,768]{1,0:T(8,128)(2,1)} fusion(bf16[90112,768]{1,0:T(8,128)(2,1)} %bitcast.18, s32[32768]{0:T(1024)S(1)} %fusion.56), kind=kCustom, calls=%fused_computation.3 | custom fusion | bytes 100794368 | tf_op jit(solution)/shard_map/jit(_take)/gather | solution.py:60
  3475.4 33.6 broadcast_select_fusion.1
  3509.0 2110.8 %gather_fusion.4 = bf16[122880,768]{1,0:T(8,128)(2,1)} fusion(bf16[32768,768]{1,0:T(8,128)(2,1)} %broadcast_select_fusion.1, s32[122880]{0:T(1024)S(1)} %copy-done.6), kind=kCustom, calls=%fused_computation.4 | custom fusion | bytes 377978880 | tf_op jit(solution)/shard_map/jit(_take)/gather | solution.py:64
  5619.8 257.9 %reshape.347 = bf16[8192,15,768]{2,1,0:T(8,128)(2,1)} reshape(bf16[122880,768]{1,0:T(8,128)(2,1)} %gather_fusion.4) | data formatting | bytes 377487360 | tf_op jit(solution)/shard_map/jit(_take)/gather | solution.py:64
  5877.7 74.8 %fusion = f32[8192,1,768]{2,1,0:T(1,128)} fusion(bf16[8192,15,1]{1,2,0:T(2,128)(2,1)} %copy.70, bf16[8192,15,768]{2,1,0:T(8,128)(2,1)} %reshape.347, pred[8192,15]{1,0:T(8,128)(4,1)S(1)} %copy-done.24), kind=kOutput, calls=%fused_computation.12 | convolution fusion | flops 283115520 | bytes 214278144 | tf_op jit(solution)/shard_map/nk,nkd->nd/dot_general | solution.py:65
  5952.5 17.5 fusion.4
  5970.0 11.3 fusion.82
  5981.3 9.3 maximum_reduce_fusion
  5991.9 2.0 copy-done.2
  5993.8 3.1 add_convert_fusion
  5996.9 6.4 copy.52
  6003.3 78.5 %gather_fusion.5 = bf16[20480,256]{1,0:T(8,128)(2,1)} fusion(bf16[8192,256]{1,0:T(8,128)(2,1)} %copy.52, s32[20480]{0:T(1024)S(1)} %copy-done.8), kind=kCustom, calls=%fused_computation.5 | custom fusion | bytes 21053440 | tf_op jit(solution)/shard_map/jit(_take)/gather | solution.py:64
  6081.8 19.5 reshape.355
  6101.4 1.8 fusion.41
  6103.2 9.7 fusion.7
  6117.5 7.6 gather_fusion.6
  6126.7 2.4 fusion.30
  6133.0 2.3 mul.241
  6135.3 3.5 mul.242
  6138.8 17.0 scatter_custom_fusion.3
  6155.8 3.4 slice_reduce_fusion
  6159.5 1.9 fusion.81
  6161.4 3.0 copy.82
  6164.4 1.9 multiply_reduce_fusion.4
  6167.0 1.8 multiply_reduce_fusion.3
  6169.7 2.4 convolution_bitcast_fusion.2
  6172.6 11.1 mul.251
  6183.7 27.9 mul.252
  6211.6 124.3 %scatter_custom_fusion.4 = f32[8192,256]{1,0:T(8,128)} fusion(s32[20480]{0:T(1024)} %reshape.404, f32[20480,256]{1,0:T(8,128)} %mul.252, f32[20480]{0:T(1024)S(1)} %copy-done.33, f32[]{:T(128)} %constant.97.clone.1), kind=kCustom, calls=%fused_computation.20 | custom fusion | flops 10485760 | bytes 29442560 | tf_op jit(solution)/shard_map/scatter-add | solution.py:73
  6335.9 6.5 slice_reduce_fusion.1
  6342.3 1.8 copy.83
  6344.2 2.5 fusion.80
  6346.6 6.6 copy.84
  6353.3 6.3 multiply_reduce_fusion.1
  6360.3 4.9 fusion.69
  6365.4 6.4 multiply_reduce_fusion
  6371.8 6.5 convolution_bitcast_fusion
  6378.3 6.5 fusion.34
  6392.7 1.7 constant_dynamic-update-slice_fusion.7
  6394.4 1.7 constant_dynamic-update-slice_fusion.6
  6400.0 1.6 constant_dynamic-update-slice_fusion.2
  6404.4 23.0 psum.21
  6428.1 29.2 all-reduce.2.cloned.1.call-done
  6457.4 7.1 divide_subtract_fusion
  (254 shorter events, 60.9 us)
Async XLA Ops:
  7.2 753.3 %copy-start = (bf16[512,768]{1,0:T(8,128)(2,1)S(1)}, bf16[512,768]{1,0:T(8,128)(2,1)}, u32[]{:S(2)}) copy-start(bf16[512,768]{1,0:T(8,128)(2,1)} %param.13) | copy-start | bytes 2359300
  760.4 369.1 %copy-start.16 = (s32[8,1,11264]{2,1,0:T(1,128)S(1)}, s32[8,1,11264]{2,1,0:T(1,128)}, u32[]{:S(2)}) copy-start(s32[8,1,11264]{2,1,0:T(1,128)} %copy-done.15) | copy-start | bytes 1081348
  1220.0 12.2 copy-start.54
  1220.0 1517.7 %copy-start.9 = (f32[604313]{0:T(1024)S(1)}, f32[604313]{0:T(1024)}, u32[]{:S(2)}) copy-start(f32[604313]{0:T(1024)} %param.23) | copy-start | bytes 7251760
  1220.0 1690.6 %all-to-all-start.1 = ((bf16[8,11264,768]{2,1,0:T(8,128)(2,1)}), bf16[8,11264,768]{2,1,0:T(8,128)(2,1)}, u32[]{:S(2)}, u32[]{:S(2)}) async-start(bf16[8,11264,768]{2,1,0:T(8,128)(2,1)} %broadcast_select_fusion), calls=%async_computation.1 | async-start | bytes 276824064 | tf_op jit(solution)/shard_map/all_to_all | solution.py:58
  1232.2 5225.1 %all-reduce.2.cloned.1.call-start = ((), (), s32[]{:S(2)}) async-start(), calls=%async_computation.2 | async-start | bytes 4841472 | tf_op jit(solution)/shard_map/psum | solution.py:162
  2742.6 5.7 copy-start.30
  2749.0 6.7 copy-start.17
  2755.7 5.3 copy-start.22
  2760.1 5.7 copy-start.31
  2762.4 9.6 copy-start.39
  2763.8 8.7 copy-start.43
  2777.3 131.1 %copy-start.40 = (s32[8192]{0:T(1024)S(1)}, s32[8192]{0:T(1024)}, u32[]{:S(2)}) copy-start(s32[8192]{0:T(1024)} %get-tuple-element.35) | copy-start | bytes 98308
  2778.3 131.5 %copy-start.18 = (s32[122880]{0:T(1024)S(1)}, s32[122880]{0:T(1024)}, u32[]{:S(2)}) copy-start(s32[122880]{0:T(1024)} %reshape.348) | copy-start | bytes 1474564
  2779.8 130.8 %copy-start.45 = (f32[2048]{0:T(1024)}, f32[2048]{0:T(1024)S(1)}, u32[]{:S(2)}) copy-start(f32[2048]{0:T(1024)S(1)} %convert_maximum_fusion.1) | copy-start | bytes 24580
  3475.4 33.6 copy-start.6
  5619.8 257.9 %copy-start.24 = (pred[8192,15]{1,0:T(8,128)(4,1)S(1)}, pred[8192,15]{1,0:T(8,128)(4,1)}, u32[]{:S(2)}) copy-start(pred[8192,15]{1,0:T(8,128)(4,1)} %copy.48) | copy-start | bytes 368644
  5877.7 74.8 %copy-start.41 = (f32[8192]{0:T(1024)S(1)}, f32[8192]{0:T(1024)}, u32[]{:S(2)}) copy-start(f32[8192]{0:T(1024)} %convert_maximum_fusion) | copy-start | bytes 98308
  5952.5 17.5 copy-start.19
  5970.0 11.3 copy-start.32
  5970.0 11.3 copy-start.67
  5990.6 3.2 copy-start.2
  5990.7 3.2 copy-start.48
  5990.7 3.2 copy-start.64
  5991.8 5.1 copy-start.34
  5996.9 6.4 copy-start.8
  6081.8 19.5 copy-start.20
  6103.2 9.7 copy-start.28
  6103.2 9.7 copy-start.46
  6103.2 9.7 copy-start.66
  6112.9 2.6 copy-start.47
  6113.0 2.6 copy-start.60
  6126.7 2.5 copy-start.51
  6126.7 2.7 copy-start.13
  6126.7 2.7 copy-start.23
  6126.7 2.9 slice-start.3
  6126.7 2.9 copy-start.21
  6130.0 5.3 copy-start.52
  6135.3 3.5 copy-start.44
  6155.8 3.4 slice-start.4
  6159.4 5.0 copy-start.5
  6164.4 1.9 copy-start.7
  6168.8 3.3 copy-start.11
  6169.7 2.4 copy-start.29
  6183.7 27.9 copy-start.33
  6335.9 6.5 slice-start.2
  6346.6 6.6 copy-start.49
  6353.2 6.3 copy-start.35
  6353.2 7.0 copy-start.3
  6353.2 11.9 slice-start
  6360.3 5.1 slice-start.1
  6378.3 6.6 copy-start.26
  6378.3 6.9 copy-start.27
  6378.3 7.4 copy-start.38
  6386.7 9.3 copy-start.63
  6386.7 10.6 copy-start.62
  6386.7 11.9 copy-start.58
  6386.8 11.9 copy-start.59
  6386.8 16.4 copy-start.61
  6388.6 15.2 copy-start.53
  6388.6 15.2 copy-start.56
  6388.6 15.2 copy-start.57
  6388.6 68.7 %copy-start.10 = (f32[604313]{0:T(1024)S(1)}, f32[604313]{0:T(1024)}, u32[]{:S(2)}) copy-start(f32[604313]{0:T(1024)} %param.23) | copy-start | bytes 7251760
  6457.4 7.1 copy-start.1
  (13 other events, 18.4 us)
Sparse Core Ops, SparseCore 0:
  6403.9 53.3 all-reduce.1
where the time goes:
time: 6530 us; the launch traced here: 6470 us
  local copies, waits for them, and re-layouts  4150 us (64%)
  blocking collectives  1540 us (24%)
  other arithmetic  586 us (9%)
  matrix products  134 us (2%)
    gather x6, local copies, waits for them, and re-layouts, neighbor_mean(): gathered = jnp.take(table, nbr_idx, axis=0)  2480 us
    psum x1, blocking collectives, local_step(): total = jnp.maximum(lax.psum(jnp.sum(valid), 'dp'), 1.0)  1500 us
    gather x1, local copies, waits for them, and re-layouts, fetch_rows(): jnp.take(returned.reshape(groups * cap, local_table.shape[1]), place, axi...  565 us
    gather x1, local copies, waits for them, and re-layouts, fetch_rows(): jnp.take(local_table, incoming.reshape(-1), axis=0)  369 us
    scatter-add x1, other arithmetic, fetch_rows(): jax.ops.segment_sum(jnp.ones_like(owner), owner, num_segments=groups)  226 us
    gather x1, local copies, waits for them, and re-layouts, fetch_rows(): sorted_owner = owner[order]  192 us
    gather x1, local copies, waits for them, and re-layouts, fetch_rows(): local_row[order]  181 us
    scatter-add x2, other arithmetic, spread_back(): jax.ops.segment_sum(contrib.reshape(-1, grad_mean.shape[1]), nbr_idx.resh...  141 us
  transfers between devices with their start and end apart: 2, of which 1 were waited for; matrix products, arithmetic and copies ran while one was open for 3% of the time, Pallas kernels for 0%

commit v1 on v0

v1 whole, which is shorter than its diff:
```python
import functools

import jax
import jax.numpy as jnp
from jax import lax
from jax.experimental import pallas as pl
from jax.experimental.pallas import tpu as pltpu
from jax.sharding import PartitionSpec as P

HIDDEN = 256
STEP = 10
LN_EPS = 1e-5
BETA_ONE = 0.9
BETA_TWO = 0.999
ADAM_LR = 3e-3
ADAM_EPS = 1e-8
F32 = jnp.float32
BF16 = jnp.bfloat16
VMEM_ALL = 60 * 1024 * 1024


def param_shapes(feat, classes):
    return [(feat, HIDDEN), (feat, HIDDEN), (HIDDEN,), (HIDDEN,), (HIDDEN,),
            (HIDDEN, HIDDEN), (HIDDEN, HIDDEN), (HIDDEN,), (HIDDEN,), (HIDDEN,),
            (HIDDEN, classes), (HIDDEN, classes), (classes,)]


def class_count(n_params, feat):
    return (n_params - 2 * feat * HIDDEN - 6 * HIDDEN - 2 * HIDDEN * HIDDEN) // (2 * HIDDEN + 1)


def unpack(flat, feat, classes):
    pieces = []
    offset = 0
    for pshape in param_shapes(feat, classes):
        count_el = 1
        for extent in pshape:
            count_el = count_el * extent
        pieces.append(flat[offset:offset + count_el].reshape(pshape))
        offset = offset + count_el
    return pieces


def params_of(*sem, vmem=VMEM_ALL):
    return pltpu.CompilerParams(dimension_semantics=sem, vmem_limit_bytes=vmem)


def emit_codes(ids, mask, shift, out_ref):
    n = ids.shape[1]
    node = lax.broadcasted_iota(jnp.int32, (16, n), 1)
    lo = (ids & 255).astype(F32)
    code = jnp.where(mask > 0, (ids >> 8) * 16 + (node & 15) - shift, -384).astype(F32)
    count = jnp.maximum(jnp.sum(mask, axis=0, keepdims=True), 1).astype(F32)
    count = jnp.broadcast_to(count, (16, n))
    for c in range(n // 128):
        lanes = slice(c * 128, (c + 1) * 128)
        stack = jnp.concatenate([lo[:, lanes], code[:, lanes], count[:, lanes],
                                 jnp.zeros((80, 128), F32)], axis=0)
        out_ref[lanes, :] = stack.T.astype(BF16)


def pad_rows(x, rows):
    return jnp.concatenate([x, jnp.zeros((rows - x.shape[0], x.shape[1]), x.dtype)], axis=0)


def compose_kernel(front_ref, nbr_ref, mask_ref, out_ref, table_ref):
    n = nbr_ref.shape[1]
    half = front_ref.shape[0] // 2

    @pl.when(pl.program_id(0) == 0)
    def _():
        table_ref[...] = front_ref[0:half, :] + (front_ref[half:2 * half, :] << 12)

    nbr = pad_rows(nbr_ref[...], 16)
    mask = pad_rows(mask_ref[...], 16)
    tiles = [(s, c) for s in range(2) for c in range(n // 128)]
    parts = [nbr[s * 8:s * 8 + 8, c * 128:c * 128 + 128] for s, c in tiles]
    lane = [part & 127 for part in parts]
    row = [part >> 7 for part in parts]
    low = [r & (half - 1) for r in row]

    def step(base, accs):
        accs = list(accs)
        block = table_ref[pl.ds(pl.multiple_of(base * 8, 8), 8), :]
        for u in range(8):
            entry = jnp.broadcast_to(block[u:u + 1, :], (8, 128))
            at = base * 8 + u
            for t in range(len(tiles)):
                got = jnp.take_along_axis(entry, lane[t], axis=1, mode="promise_in_bounds")
                accs[t] = jnp.where(low[t] == at, got, accs[t])
        return tuple(accs)

    accs = lax.fori_loop(0, half // 8, step, tuple(jnp.zeros((8, 128), jnp.int32) for _ in tiles))
    ids = [jnp.where(row[t] >= half, accs[t] >> 12, accs[t]) & 4095 for t in range(len(tiles))]
    cols = n // 128
    ids = jnp.concatenate([jnp.concatenate(ids[s * cols:(s + 1) * cols], axis=1) for s in range(2)], axis=0)
    emit_codes(ids, mask, 0, out_ref)


def codes_kernel(shift, nbr_ref, mask_ref, out_ref):
    emit_codes(pad_rows(nbr_ref[...], 16), pad_rows(mask_ref[...], 16), shift, out_ref)


def compose(frontier, nbr_t, mask_t, block=512):
    n = nbr_t.shape[1]
    rows = frontier.shape[0] // 128
    return pl.pallas_call(
        compose_kernel,
        grid=(n // block,),
        in_specs=[pl.BlockSpec((rows, 128), lambda i: (0, 0)),
                  pl.BlockSpec((nbr_t.shape[0], block), lambda i: (0, i)),
                  pl.BlockSpec((nbr_t.shape[0], block), lambda i: (0, i))],
        out_specs=pl.BlockSpec((block, 128), lambda i: (i, 0)),
        out_shape=jax.ShapeDtypeStruct((n, 128), BF16),
        scratch_shapes=[pltpu.VMEM((rows // 2, 128), jnp.int32)],
        compiler_params=params_of("arbitrary"),
        cost_estimate=pl.CostEstimate(flops=10**9, bytes_accessed=10**7, transcendentals=0),
        name="compose_ids",
    )(frontier.reshape(rows, 128), nbr_t, mask_t)


def codes(nbr_t, mask_t, shift, block=512):
    n = nbr_t.shape[1]
    return pl.pallas_call(
        functools.partial(codes_kernel, shift),
        grid=(n // block,),
        in_specs=[pl.BlockSpec((nbr_t.shape[0], block), lambda i: (0, i)),
                  pl.BlockSpec((nbr_t.shape[0], block), lambda i: (0, i))],
        out_specs=pl.BlockSpec((block, 128), lambda i: (i, 0)),
        out_shape=jax.ShapeDtypeStruct((n, 128), BF16),
        compiler_params=params_of("arbitrary"),
        name="codes",
    )(nbr_t, mask_t)


def count_kernel(fan, halves, unroll, codes_ref, out_ref):
    nodes = codes_ref.shape[0]
    lane = lax.broadcasted_iota(jnp.int32, (16, 256), 1).astype(F32).astype(BF16)
    one = jnp.ones((16, 256), BF16)
    zero = jnp.zeros((16, 256), BF16)

    def group(g):
        at = pl.multiple_of(g * 16, 16)
        block = codes_ref[pl.ds(at, 16), :]
        low = [jnp.where(lane == block[:, k:k + 1], one, zero) for k in range(fan)]
        low = jnp.concatenate(low + [zero] * (16 - fan), axis=0)
        for h in range(halves):
            want = lane if h == halves - 1 else lane - 256
            high = [jnp.where(want == block[:, 16 + k:17 + k], one, zero) for k in range(fan)]
            high = jnp.concatenate(high + [zero] * (16 - fan), axis=0)
            got = lax.dot_general(high, low, (((0,), (0,)), ((), ())), preferred_element_type=F32).astype(BF16)
            for p in range(16):
                out_ref[pl.ds(at, 16), (h * 16 + p) * 256:(h * 16 + p + 1) * 256] = got[p * 16:p * 16 + 16, :]

    def step(s, carry):
        for u in range(unroll):
            group(s * unroll + u)
        return carry

    lax.fori_loop(0, nodes // (16 * unroll), step, 0)


def count_matrix(code, fan, vocab, block=256, unroll=4):
    n = code.shape[0]
    return pl.pallas_call(
        functools.partial(count_kernel, fan, vocab // 4096, unroll),
        grid=(n // block,),
        in_specs=[pl.BlockSpec((block, 128), lambda i: (i, 0))],
        out_specs=pl.BlockSpec((block, vocab), lambda i: (i, 0)),
        out_shape=jax.ShapeDtypeStruct((n, vocab), BF16),
        compiler_params=params_of("arbitrary"),
        cost_estimate=pl.CostEstimate(flops=2 * n * vocab * 256, bytes_accessed=2 * n * vocab, transcendentals=0),
        name="count_matrix",
    )(code)


def norm_rows(z, gain, shift):
    act = jnp.maximum(z, 0.0)
    mean_act = jnp.mean(act, axis=-1, keepdims=True)
    centred = act - mean_act
    var_act = jnp.mean(centred * centred, axis=-1, keepdims=True)
    return centred * lax.rsqrt(var_act + LN_EPS) * gain + shift


def norm_back(z, gain, d_out, axis):
    act = jnp.maximum(z, 0.0)
    mean_act = jnp.mean(act, axis=axis, keepdims=True)
    centred = act - mean_act
    var_act = jnp.mean(centred * centred, axis=axis, keepdims=True)
    inv = lax.rsqrt(var_act + LN_EPS)
    hat = centred * inv
    d_hat = d_out * gain
    mean_d = jnp.mean(d_hat, axis=axis, keepdims=True)
    mean_dh = jnp.mean(d_hat * hat, axis=axis, keepdims=True)
    d_act = (d_hat - mean_d - hat * mean_dh) * inv
    return jnp.where(z > 0.0, d_act, 0.0), d_out * hat


def layer_one_kernel(self_ids, m_ref, codes_ref, x_ref, w_self_ref, w_nbr_ref, vec_ref,
                     hs_ref, a_ref, h_ref, zt_ref, wide_ref, got_ref):
    block = m_ref.shape[0]
    rows, feat = x_ref.shape
    pid = pl.program_id(0)
    tiles = feat // 128

    @pl.when(pid == 0)
    def _():
        def spread(s, carry):
            at = pl.multiple_of(s * 128, 128)
            for c in range(tiles):
                wide_ref[pl.ds(at * 8 + c, 128, stride=8), :] = x_ref[pl.ds(at, 128), c * 128:(c + 1) * 128].astype(F32)
            return carry
        lax.fori_loop(0, rows // 128, spread, 0)

    def fetch(s, carry):
        for u in range(32):
            at = s * 32 + u
            idx = self_ids[pid * block + at]
            got_ref[pl.ds(pl.multiple_of(at * 8, 8), 8), :] = wide_ref[pl.ds(pl.multiple_of(idx * 8, 8), 8), :]
        return carry
    lax.fori_loop(0, block // 32, fetch, 0)
    for c in range(tiles):
        hs_ref[:, c * 128:(c + 1) * 128] = got_ref[pl.ds(c, block, stride=8), :].astype(BF16)
    count = codes_ref[:, 32:33].astype(F32)
    for c in range(feat // 256):
        cols = slice(c * 256, (c + 1) * 256)
        acc = jnp.dot(m_ref[...], x_ref[:, cols], preferred_element_type=F32)
        a_ref[:, cols] = (acc / count).astype(BF16)
    z = (jnp.dot(hs_ref[...], w_self_ref[...], preferred_element_type=F32)
         + jnp.dot(a_ref[...], w_nbr_ref[...], preferred_element_type=F32) + vec_ref[0:1, :])
    h_ref[...] = norm_rows(z, vec_ref[1:2, :], vec_ref[2:3, :]).astype(BF16)
    zt_ref[...] = z.T


def layer_one(m_one, code, table, self_ids, w_self, w_nbr, vecs, block=512):
    n, rows = m_one.shape
    feat = table.shape[1]
    whole = lambda i, ids: (0, 0)
    by_row = lambda i, ids: (i, 0)
    return pl.pallas_call(
        layer_one_kernel,
        grid_spec=pltpu.PrefetchScalarGridSpec(
            num_scalar_prefetch=1,
            grid=(n // block,),
            in_specs=[pl.BlockSpec((block, rows), by_row),
                      pl.BlockSpec((block, 128), by_row),
                      pl.BlockSpec((rows, feat), whole),
                      pl.BlockSpec((feat, HIDDEN), whole),
                      pl.BlockSpec((feat, HIDDEN), whole),
                      pl.BlockSpec((8, HIDDEN), whole)],
            out_specs=[pl.BlockSpec((block, feat), by_row),
                       pl.BlockSpec((block, feat), by_row),
                       pl.BlockSpec((block, HIDDEN), by_row),
                       pl.BlockSpec((HIDDEN, block), lambda i, ids: (0, i))],
            scratch_shapes=[pltpu.VMEM((rows * 8, 128), F32), pltpu.VMEM((block * 8, 128), F32)]),
        out_shape=[jax.ShapeDtypeStruct((n, feat), BF16),
                   jax.ShapeDtypeStruct((n, feat), BF16),
                   jax.ShapeDtypeStruct((n, HIDDEN), BF16),
                   jax.ShapeDtypeStruct((HIDDEN, n), F32)],
        compiler_params=params_of("arbitrary"),
        cost_estimate=pl.CostEstimate(flops=2 * n * rows * feat, bytes_accessed=2 * n * rows, transcendentals=0),
        name="layer_one",
    )(self_ids, m_one, code, table, w_self, w_nbr, vecs)


def layer_two_kernel(m_ref, codes_ref, h_all_ref, h_self_ref, w_self_ref, w_nbr_ref, vec_ref, a_ref, h_ref, z_ref):
    count = codes_ref[:, 32:33].astype(F32)
    acc = jnp.dot(m_ref[...], h_all_ref[...], preferred_element_type=F32)
    a_ref[...] = (acc / count).astype(BF16)
    z = (jnp.dot(h_self_ref[...], w_self_ref[...], preferred_element_type=F32)
         + jnp.dot(a_ref[...], w_nbr_ref[...], preferred_element_type=F32) + vec_ref[0:1, :])
    z_ref[...] = z
    h_ref[...] = norm_rows(z, vec_ref[1:2, :], vec_ref[2:3, :]).astype(BF16)


def layer_two(m_two, code, h_one, w_self, w_nbr, vecs, block=512):
    n, rows = m_two.shape
    whole = lambda i: (0, 0)
    by_row = lambda i: (i, 0)
    return pl.pallas_call(
        layer_two_kernel,
        grid=(n // block,),
        in_specs=[pl.BlockSpec((block, rows), by_row),
                  pl.BlockSpec((block, 128), by_row),
                  pl.BlockSpec((rows, HIDDEN), whole),
                  pl.BlockSpec((block, HIDDEN), by_row),
                  pl.BlockSpec((HIDDEN, HIDDEN), whole),
                  pl.BlockSpec((HIDDEN, HIDDEN), whole),
                  pl.BlockSpec((8, HIDDEN), whole)],
        out_specs=[pl.BlockSpec((block, HIDDEN), by_row)] * 3,
        out_shape=[jax.ShapeDtypeStruct((n, HIDDEN), BF16),
                   jax.ShapeDtypeStruct((n, HIDDEN), BF16),
                   jax.ShapeDtypeStruct((n, HIDDEN), F32)],
        compiler_params=params_of("arbitrary"),
        cost_estimate=pl.CostEstimate(flops=2 * n * rows * HIDDEN, bytes_accessed=2 * n * rows, transcendentals=0),
        name="layer_two",
    )(m_two, code, h_one, h_one, w_self, w_nbr, vecs)


def tdot(lhs, rhs):
    return lax.dot_general(lhs, rhs, (((0,), (0,)), ((), ())), preferred_element_type=F32)


def dot_t(lhs, rhs):
    return lax.dot_general(lhs, rhs, (((1,), (1,)), ((), ())), preferred_element_type=F32)


def top_kernel(classes, nbr3_ref, mask3_ref, label_ref, valid_ref, h2_ref, a2_ref, z2_ref, h1_ref, codes2_ref,
               w3s_ref, w3n_ref, w2s_ref, w2n_ref, vec_ref,
               g3s_ref, g3n_ref, g2s_ref, g2n_ref, vout_ref, dself_ref, dagg_ref, m3_ref, dh2_ref):
    seeds = nbr3_ref.shape[0]
    n_two = h2_ref.shape[0]
    fan = nbr3_ref.shape[1]
    piece = 512
    count3 = jnp.maximum(jnp.sum(mask3_ref[...], axis=1, keepdims=True), 1).astype(F32)
    for c in range(n_two // piece):
        ids = lax.broadcasted_iota(jnp.int32, (seeds, piece), 1) + c * piece
        acc = jnp.zeros((seeds, piece), F32)
        for k in range(fan):
            want = jnp.where(mask3_ref[:, k:k + 1] > 0, nbr3_ref[:, k:k + 1], -1)
            acc = acc + jnp.where(ids == want, 1.0, 0.0)
        m3_ref[:, c * piece:(c + 1) * piece] = acc.astype(BF16)
    a3 = (jnp.dot(m3_ref[...], h2_ref[...], preferred_element_type=F32) / count3).astype(BF16)
    self3 = h2_ref[0:seeds, :]
    logits = (jnp.dot(self3, w3s_ref[...], preferred_element_type=F32)
              + jnp.dot(a3, w3n_ref[...], preferred_element_type=F32) + vec_ref[3:4, :])
    col = lax.broadcasted_iota(jnp.int32, logits.shape, 1)
    real = col < classes
    top = jnp.max(jnp.where(real, logits, -jnp.inf), axis=1, keepdims=True)
    powers = jnp.where(real, jnp.exp(logits - top), 0.0)
    total = jnp.sum(powers, axis=1, keepdims=True)
    log_norm = top + jnp.log(total)
    hot = col == label_ref[...]
    picked = jnp.sum(jnp.where(hot, logits, 0.0), axis=1, keepdims=True)
    valid = valid_ref[...].astype(F32)
    loss = jnp.sum((log_norm - picked) * valid, axis=0, keepdims=True)
    n_valid = jnp.sum(valid, axis=0, keepdims=True)
    d_logits = (jnp.where(real, jnp.exp(logits - log_norm), 0.0) - jnp.where(hot, 1.0, 0.0)) * valid
    d_logb = d_logits.astype(BF16)
    g3s_ref[...] = tdot(self3, d_logb)
    g3n_ref[...] = tdot(a3, d_logb)
    d_self3 = dot_t(d_logb, w3s_ref[...])
    d_agg3 = (dot_t(d_logb, w3n_ref[...]) / count3).astype(BF16)
    dh2_ref[...] = tdot(m3_ref[...], d_agg3)
    dh2_ref[0:seeds, :] += d_self3
    d_h2 = dh2_ref[...]
    d_z2, gain_terms = norm_back(z2_ref[...], vec_ref[1:2, :], d_h2, -1)
    vout_ref[0:1, :] = jnp.sum(d_z2, axis=0, keepdims=True)
    vout_ref[1:2, :] = jnp.sum(gain_terms, axis=0, keepdims=True)
    vout_ref[2:3, :] = jnp.sum(d_h2, axis=0, keepdims=True)
    vout_ref[3:4, :] = jnp.sum(d_logits, axis=0, keepdims=True)
    vout_ref[4:5, :] = jnp.broadcast_to(loss, (1, HIDDEN))
    vout_ref[5:6, :] = jnp.broadcast_to(n_valid, (1, HIDDEN))
    vout_ref[6:8, :] = jnp.zeros((2, HIDDEN), F32)
    d_z2b = d_z2.astype(BF16)
    g2s_ref[...] = tdot(h1_ref[...], d_z2b)
    g2n_ref[...] = tdot(a2_ref[...], d_z2b)
    dself_ref[...] = dot_t(d_z2b, w2s_ref[...]).T
    count2 = codes2_ref[:, 32:33].astype(F32)
    dagg_ref[...] = (dot_t(d_z2b, w2n_ref[...]) / count2).T.astype(BF16)


def top(classes, nbr3, mask3, label, valid, h2, a2, z2, h1, codes2, w3s, w3n, w2s, w2n, vecs):
    n_two = h2.shape[0]
    seeds = nbr3.shape[0]
    square = jax.ShapeDtypeStruct((HIDDEN, HIDDEN), F32)
    full = lambda x: pl.BlockSpec(x.shape, lambda i: (0, 0))
    args = (nbr3, mask3, label, valid, h2, a2, z2, h1, codes2, w3s, w3n, w2s, w2n, vecs)
    outs = [square, square, square, square, jax.ShapeDtypeStruct((8, HIDDEN), F32),
            jax.ShapeDtypeStruct((HIDDEN, n_two), F32), jax.ShapeDtypeStruct((HIDDEN, n_two), BF16)]
    specs = [full(x) for x in args]
    specs[7] = pl.BlockSpec((n_two, HIDDEN), lambda i: (0, 0))
    return pl.pallas_call(
        functools.partial(top_kernel, classes),
        grid=(1,),
        in_specs=specs,
        out_specs=[full(x) for x in outs],
        out_shape=outs,
        scratch_shapes=[pltpu.VMEM((seeds, n_two), BF16), pltpu.VMEM((n_two, HIDDEN), F32)],
        compiler_params=params_of("arbitrary"),
        name="layer_three",
    )(*args)


def bottom_kernel(dagg_ref, m_ref, dself_ref, zt_ref, hs_ref, a_ref, gain_ref,
                  gs_ref, gn_ref, vout_ref):
    pid = pl.program_id(0)
    block = m_ref.shape[1]
    n_self = dself_ref.shape[1] // block

    @pl.when(pid == 0)
    def _():
        gs_ref[...] = jnp.zeros_like(gs_ref)
        gn_ref[...] = jnp.zeros_like(gn_ref)
        vout_ref[...] = jnp.zeros_like(vout_ref)

    d_h = jnp.dot(dagg_ref[...], m_ref[...], preferred_element_type=F32)
    at = pl.multiple_of(jnp.minimum(pid, n_self - 1) * block, block)
    d_h = d_h + jnp.where(pid < n_self, dself_ref[:, pl.ds(at, block)], 0.0)
    d_z, gain_terms = norm_back(zt_ref[...], gain_ref[:, 0:1], d_h, 0)
    sums = [jnp.sum(term, axis=1, keepdims=True) for term in (d_z, gain_terms, d_h)]
    lane = lax.broadcasted_iota(jnp.int32, (HIDDEN, 128), 1)
    vout_ref[...] += jnp.where(lane == 0, sums[0], jnp.where(lane == 1, sums[1], jnp.where(lane == 2, sums[2], 0.0)))
    d_zb = d_z.astype(BF16)
    gs_ref[...] += jnp.dot(d_zb, hs_ref[...], preferred_element_type=F32)
    gn_ref[...] += jnp.dot(d_zb, a_ref[...], preferred_element_type=F32)


def bottom(dagg_t, m_two, dself_t, z_t, h_self, a_one, gain_col, block=512):
    n_two, n = m_two.shape
    feat = h_self.shape[1]
    whole = lambda i: (0, 0)
    grads = jax.ShapeDtypeStruct((HIDDEN, feat), F32)
    return pl.pallas_call(
        bottom_kernel,
        grid=(n // block,),
        in_specs=[pl.BlockSpec((HIDDEN, n_two), whole),
                  pl.BlockSpec((n_two, block), lambda i: (0, i)),
                  pl.BlockSpec((HIDDEN, n_two), whole),
                  pl.BlockSpec((HIDDEN, block), lambda i: (0, i)),
                  pl.BlockSpec((block, feat), lambda i: (i, 0)),
                  pl.BlockSpec((block, feat), lambda i: (i, 0)),
                  pl.BlockSpec((HIDDEN, 128), whole)],
        out_specs=[pl.BlockSpec((HIDDEN, feat), whole), pl.BlockSpec((HIDDEN, feat), whole),
                   pl.BlockSpec((HIDDEN, 128), whole)],
        out_shape=[grads, grads, jax.ShapeDtypeStruct((HIDDEN, 128), F32)],
        compiler_params=params_of("arbitrary"),
        cost_estimate=pl.CostEstimate(flops=2 * n * n_two * HIDDEN, bytes_accessed=2 * n * n_two, transcendentals=0),
        name="layer_one_back",
    )(dagg_t, m_two, dself_t, z_t, h_self, a_one, gain_col)


def adam_update(params, adam_m, adam_v, grads):
    m_new = BETA_ONE * adam_m + (1.0 - BETA_ONE) * grads
    v_new = BETA_TWO * adam_v + (1.0 - BETA_TWO) * grads * grads
    m_hat = m_new / (1.0 - BETA_ONE ** STEP)
    v_hat = v_new / (1.0 - BETA_TWO ** STEP)
    return (params - ADAM_LR * m_hat / (jnp.sqrt(v_hat) + ADAM_EPS), m_new, v_new)


def stack_rows(*rows):
    width = HIDDEN
    rows = [jnp.pad(row, (0, width - row.shape[0])) for row in rows]
    rows += [jnp.zeros((width,), F32)] * (8 - len(rows))
    return jnp.stack(rows)


def solution(mesh):
    def body(feats, frontier, nbr_l1, mask_l1, nbr_l2, mask_l2, nbr_l3, mask_l3, labels, seed_mask, params, adam_m, adam_v):
        feat = feats.shape[1]
        classes = class_count(params.shape[0], feat)
        n_one = nbr_l1.shape[0]
        table = lax.all_gather(feats, 'dp', axis=0, tiled=True)
        pieces = unpack(params, feat, classes)
        pad3 = ((0, 0), (0, HIDDEN - classes))
        w3s = jnp.pad(pieces[10], pad3).astype(BF16)
        w3n = jnp.pad(pieces[11], pad3).astype(BF16)
        code_one = compose(frontier, nbr_l1.T, mask_l1.T)
        code_two = codes(nbr_l2.T, mask_l2.T, 256)
        m_one = count_matrix(code_one, nbr_l1.shape[1], table.shape[0])
        m_two = count_matrix(code_two, nbr_l2.shape[1], n_one)
        h_self, a_one, h_one, z_one_t = layer_one(
            m_one, code_one, table, frontier[:n_one], pieces[0].astype(BF16), pieces[1].astype(BF16),
            stack_rows(pieces[2], pieces[3], pieces[4]))
        a_two, h_two, z_two = layer_two(m_two, code_two, h_one, pieces[5].astype(BF16), pieces[6].astype(BF16),
                                        stack_rows(pieces[7], pieces[8], pieces[9]))
        g3s, g3n, g2s, g2n, vout, dself_t, dagg_t = top(
            classes, nbr_l3, mask_l3, labels[:, None], seed_mask[:, None], h_two, a_two, z_two, h_one, code_two,
            w3s, w3n, pieces[5].astype(BF16), pieces[6].astype(BF16),
            stack_rows(pieces[7], pieces[8], pieces[9], pieces[12]))
        gain_col = jnp.broadcast_to(pieces[3][:, None], (HIDDEN, 128))
        g1s, g1n, vone = bottom(dagg_t, m_two, dself_t, z_one_t, h_self, a_one, gain_col)
        sums = jnp.concatenate([
            g1s.T.reshape(-1), g1n.T.reshape(-1), vone[:, 0], vone[:, 1], vone[:, 2],
            g2s.reshape(-1), g2n.reshape(-1), vout[0], vout[1], vout[2],
            g3s[:, :classes].reshape(-1), g3n[:, :classes].reshape(-1), vout[3, :classes],
            vout[4, :1], vout[5, :1]])
        sums = lax.psum(sums, 'dp')
        total = jnp.maximum(sums[-1], 1.0)
        loss = sums[-2] / total
        return (loss,) + adam_update(params, adam_m, adam_v, sums[:-2] / total)

    row_spec = P('dp')
    replicated = P()
    return jax.shard_map(body, mesh=mesh, in_specs=(row_spec,) * 10 + (replicated,) * 3,
                         out_specs=(replicated,) * 4, check_vma=False)
```

time: 6530 us -> 523 us (0.08)
  local copies, waits for them, and re-layouts: 4150 us -> 58.6 us
  blocking collectives: 1540 us -> 0 us
  other arithmetic: 586 us -> 8.95 us
  Pallas kernels: 0 us -> 381 us
  matrix products: 134 us -> 0 us
    gather x11 -> x0, local copies, waits for them, and re-layouts: 3780 us -> none  [the longest x6 2480 us: neighbor_mean(): gathered = jnp.take(table, nbr_idx, axis=0)]
    psum x2 -> x0, blocking collectives: 1530 us -> none  [the longest x1 1500 us: local_step(): total = jnp.maximum(lax.psum(jnp.sum(valid), 'dp'), 1.0)]
    pallas_call x0 -> x8, Pallas kernels: none -> 381 us  [the longest x2 146 us: count_matrix(): pl.pallas_call(functools.partial(count_kernel, fan, vocab // 4096, unroll...]
    scatter-add x3 -> x0, other arithmetic: 368 us -> none  [the longest x1 226 us: fetch_rows(): jax.ops.segment_sum(jnp.ones_like(owner), owner, num_segments=groups)]
    scatter x2 -> x0, local copies, waits for them, and re-layouts: 240 us -> none  [the longest x1 120 us: fetch_rows(): jnp.zeros((groups * cap,), jnp.int32).at[slot].set(local_row[order])]
    dot_general x19 -> x0, matrix products: 134 us -> none  [the longest x3 86.9 us: neighbor_mean(): jnp.einsum('nk,nkd->nd', nbr_mask.astype(jnp.bfloat16), gathered, preferr...]
    select_n x9 -> x0, other arithmetic: 126 us -> none  [the longest x2 90.8 us: fetch_rows(): jnp.take(local_table, incoming.reshape(-1), axis=0)]
  transfers between devices with their start and end apart: 2 -> 2, of which waited for: 1 -> 1; matrix products, arithmetic and copies ran while one was open for 3% -> 3% of each run, Pallas kernels for 0% -> 41%
where the time goes in v1:
time: 523 us; the launch traced here: 521 us
  Pallas kernels  381 us (73%)
  local copies, waits for them, and re-layouts  58.6 us (11%)
  waiting for transfers between devices  55.8 us (11%)
  between operations  16.6 us (3%)
  other arithmetic  8.95 us (2%)
    pallas_call x2, Pallas kernels, count_matrix(): pl.pallas_call(functools.partial(count_kernel, fan, vocab // 4096, unroll...  146 us
    pallas_call x1, Pallas kernels, layer_one(): pl.pallas_call(layer_one_kernel, grid_spec=pltpu.PrefetchScalarGridSpec(n...  98.1 us
    pallas_call x1, Pallas kernels, compose(): pl.pallas_call(compose_kernel, grid=(n // block,), in_specs=[pl.BlockSpec...  66.7 us
    psum x1, waiting for transfers between devices, body(): sums = lax.psum(sums, 'dp')  55.1 us
    pallas_call x1, Pallas kernels, bottom(): pl.pallas_call(bottom_kernel, grid=(n // block,), in_specs=[pl.BlockSpec(...  33.8 us
    concatenate x1, local copies, waits for them, and re-layouts, body(): jnp.concatenate([g1s.T.reshape(-1), g1n.T.reshape(-1), vone[:, 0], vone[:...  27.2 us
    pallas_call x1, Pallas kernels, layer_two(): pl.pallas_call(layer_two_kernel, grid=(n // block,), in_specs=[pl.BlockSp...  20.8 us
    pallas_call x1, Pallas kernels, top(): pl.pallas_call(functools.partial(top_kernel, classes), grid=(1,), in_spec...  12.4 us
  transfers between devices with their start and end apart: 2, of which 1 were waited for; matrix products, arithmetic and copies ran while one was open for 3% of the time, Pallas kernels for 41%

profile of v1, /device:TPU:0, one launch (start us, length us, event | category | flops | bytes accessed | tf_op | source)
XLA Modules:
  0.0 521.5 jit_solution(3445270013773982623)
XLA Ops:
  7.2 0.0 all-gather.2.cloned.1.call-start
  7.2 0.7 all-gather.2.cloned.1.call-update
  7.9 0.0 all-reduce.5.cloned.1.call-start
  7.9 1.8 convert.14
  9.8 0.0 copy-start.1
  9.8 0.0 slice-start
  9.8 0.0 copy-start
  9.8 1.0 copy-done.1
  10.8 0.1 fusion.6
  10.8 0.0 copy-start.6
  10.8 0.0 copy-start.7
  10.9 0.0 copy-start.8
  10.9 0.9 convert_element_type.21.w_self_ref
  11.7 0.9 convert_element_type.22.w_nbr_ref
  12.6 1.4 slice.90.self_ids
  14.0 1.0 fusion.5
  15.0 0.7 convert_element_type.23.w_self_ref.w2s_ref
  15.7 0.7 convert_element_type.24.w_nbr_ref.w2n_ref
  16.4 0.0 slice-done
  16.4 0.0 copy-done
  16.5 0.6 stack.40.vec_ref
  17.1 0.6 stack.42.vec_ref
  17.7 1.0 fusion.4
  18.7 0.4 reshape.49
  19.1 0.4 reshape.50
  19.4 0.7 pad.13.w3s_ref
  20.1 0.7 pad.14.w3n_ref
  20.8 0.0 copy-done.5
  20.8 0.8 copy.19.nbr3_ref
  21.6 0.0 copy-done.6
  21.6 0.8 copy.20.mask3_ref
  22.5 0.0 copy-done.7
  22.5 0.9 copy.21.label_ref
  23.4 0.0 copy-done.8
  23.4 0.9 copy.22.valid_ref
  24.2 3.1 codes.1.codes_ref.codes2_ref
  27.3 0.6 stack.36.vec_ref
  27.9 66.7 %compose_ids.1.codes_ref = bf16[8192,128]{1,0:T(8,128)(2,1)} custom-call(s32[256,128]{1,0:T(8,128)} %bitcast.55, s32[15,8192]{1,0:T(8,128)} %bitcast.65, s32[15,8192]{1,0:T(8,128)} %bitcast.66), custom_call_target="tpu_custom_call" | custom-call | flops 1000000000 | bytes 10000000 | tf_op jit(solution)/shard_map/compose_ids/pallas_call | solution.py:107
  94.6 33.4 %count_matrix.2.m_ref = bf16[2048,8192]{1,0:T(8,128)(2,1)} custom-call(bf16[2048,128]{1,0:T(8,128)(2,1)} %codes.1.codes_ref.codes2_ref), custom_call_target="tpu_custom_call" | custom-call | flops 8589934592 | bytes 33554432 | tf_op jit(solution)/shard_map/count_matrix/pallas_call | solution.py:165
  128.0 113.1 %count_matrix.3.m_ref = bf16[8192,4096]{1,0:T(8,128)(2,1)} custom-call(bf16[8192,128]{1,0:T(8,128)(2,1)} %compose_ids.1.codes_ref), custom_call_target="tpu_custom_call" | custom-call | flops 17179869184 | bytes 67108864 | tf_op jit(solution)/shard_map/count_matrix/pallas_call | solution.py:165
  241.1 98.1 %layer_one.1 = (bf16[8192,768]{1,0:T(8,128)(2,1)}, bf16[8192,768]{1,0:T(8,128)(2,1)}, bf16[8192,256]{1,0:T(8,128)(2,1)}, f32[256,8192]{1,0:T(8,128)}) custom-call(s32[8192]{0:T(1024)} %slice.90.self_ids, bf16[8192,4096]{1,0:T(8,128)(2,1)} %count_matrix.3.m_ref, bf16[8192,128]{1,0:T(8,128)(2,1)} %compose_ids.1.codes_ref, ...), custom_call_target="tpu_custom_call" | custom-call | flops 51539607552 | bytes 67108864 | tf_op jit(solution)/shard_map/layer_one/pallas_call | solution.py:240
  339.3 20.8 %layer_two.1 = (bf16[2048,256]{1,0:T(8,128)(2,1)}, bf16[2048,256]{1,0:T(8,128)(2,1)}, f32[2048,256]{1,0:T(8,128)}) custom-call(bf16[2048,8192]{1,0:T(8,128)(2,1)} %count_matrix.2.m_ref, bf16[2048,128]{1,0:T(8,128)(2,1)} %codes.1.codes_ref.codes2_ref, bf16[8192,256]{1,0:T(8,128)(2,1)} %get-tuple-element.21.h_all_ref.h_self_ref.h1_ref, ...), custom_call_target="tpu_custom_call" | custom-call | flops 8589934592 | bytes 33554432 | tf_op jit(solution)/shard_map/layer_two/pallas_call | solution.py:280
  360.1 12.4 %layer_three.1 = (f32[256,256]{1,0:T(8,128)}, f32[256,256]{1,0:T(8,128)}, f32[256,256]{1,0:T(8,128)}, f32[256,256]{1,0:T(8,128)}, f32[8,256]{1,0:T(8,128)}, /*in...) custom-call(s32[512,5]{1,0:T(8,128)} %copy.19.nbr3_ref, s32[512,5]{1,0:T(8,128)} %copy.20.mask3_ref, s32[512,1]{1,0:T(8,128)} %copy.21.label_ref, ...), custom_call_target="tpu_custom_call" | custom-call | tf_op jit(solution)/shard_map/layer_three/pallas_call | solution.py:373
  372.5 0.8 fusion.8
  373.3 1.3 fusion.7
  374.6 0.7 slice.112
  375.3 0.8 broadcast_in_dim.14.gain_ref
  376.1 33.8 %layer_one_back.1 = (f32[256,768]{1,0:T(8,128)}, f32[256,768]{1,0:T(8,128)}, f32[256,128]{1,0:T(8,128)}) custom-call(bf16[256,2048]{1,0:T(8,128)(2,1)} %get-tuple-element.25.dagg_ref, bf16[2048,8192]{1,0:T(8,128)(2,1)} %count_matrix.2.m_ref, f32[256,2048]{1,0:T(8,128)} %get-tuple-element.26.dself_ref, f32[256,8192]{1,0:T(8,128)} %get-tuple-element.27.zt_ref, ...), custom_call_target="tpu_custom_call" | custom-call | flops 8589934592 | bytes 33554432 | tf_op jit(solution)/shard_map/layer_one_back/pallas_call | solution.py:414
  409.9 1.4 copy.23
  411.3 0.0 copy-start.3
  411.3 1.3 copy.25
  412.6 1.4 copy.24
  414.0 1.3 copy.26
  415.3 0.0 copy-done.3
  415.3 0.3 slice_reduce_fusion
  415.6 1.1 copy.27
  416.7 0.8 copy.28
  417.5 2.0 reshape.55
  419.5 2.0 reshape.56
  421.4 27.2 %concatenate.3 = f32[604315]{0:T(1024)} concatenate(f32[196608]{0:T(1024)S(1)} %bitcast.36, f32[196608]{0:T(1024)} %bitcast.37, f32[256]{0:T(256)S(1)} %get-tuple-element.40, f32[256]{0:T(256)S(1)} %get-tuple-element.39, f32[256]{0:T(256)S(1)} %get-tuple-element.38, f32[65536]{0:T(1024)S(1)} %bitcast.38, f32[65536]{0:T(1024)} %bitcast.39, f32[256]{0:T(256)S(1)} %bitcast.62, ...), dimensions={0} | concatenate | bytes 4834520 | tf_op jit(solution)/shard_map/concatenate | solution.py:473
  448.6 0.0 all-reduce.5.cloned.1.call-update
  448.6 55.1 %all-reduce.5.cloned.1.call-done = f32[604315]{0:T(1024)} async-done(((f32[604315]{0:T(1024)}), f32[604315]{0:T(1024)}) %all-reduce.5.cloned.1.call-update) | async-done | bytes 2417276 | tf_op jit(solution)/shard_map/psum | solution.py:478
  503.7 1.3 fusion.2
  506.4 7.1 %divide_subtract_fusion = (f32[604313]{0:T(1024)}, f32[604313]{0:T(1024)}, f32[604313]{0:T(1024)}) fusion(f32[604313]{0:T(1024)S(1)} %copy-done, f32[]{:T(128)} %bitcast.23, f32[604315]{0:T(1024)} %all-reduce.5.cloned.1.call-done, f32[604313]{0:T(1024)} %param.24, f32[604313]{0:T(1024)} %param.25), kind=kLoop, calls=%fused_computation.3 | loop fusion | flops 7856069 | bytes 16920768 | tf_op jit(solution)/shard_map/sub | solution.py:438
  (10 shorter events, 0.0 us)
Async XLA Ops:
  7.2 234.0 %all-gather.2.cloned.1.call-start = ((), (), s32[]{:S(2)}) async-start(), calls=%async_computation | async-start | bytes 7077888 | tf_op jit(solution)/shard_map/all_gather | solution.py:453
  7.9 495.8 %all-reduce.5.cloned.1.call-start = ((), (), s32[]{:S(2)}) async-start(), calls=%async_computation.1 | async-start | bytes 4841472 | tf_op jit(solution)/shard_map/psum | solution.py:478
  9.8 1.0 copy-start.1
  9.8 6.7 %slice-start = ((f32[604313]{0:T(1024)}), f32[153]{0:T(256)S(1)}, s32[]{:S(2)}) async-start(f32[604313]{0:T(1024)} %param.23), calls=%async_computation.2 | async-start | bytes 2048 | tf_op jit(solution)/shard_map/slice | solution.py:39
  9.8 6.7 %copy-start = (f32[604313]{0:T(1024)S(1)}, f32[604313]{0:T(1024)}, u32[]{:S(2)}) copy-start(f32[604313]{0:T(1024)} %param.23) | copy-start | bytes 7251760
  10.8 10.0 %copy-start.5 = (s32[512,5]{0,1:T(8,128)S(1)}, s32[512,5]{0,1:T(8,128)}, u32[]{:S(2)}) copy-start(s32[512,5]{0,1:T(8,128)} %param.19) | copy-start | bytes 30724
  10.8 10.8 %copy-start.6 = (s32[512,5]{0,1:T(8,128)S(1)}, s32[512,5]{0,1:T(8,128)}, u32[]{:S(2)}) copy-start(s32[512,5]{0,1:T(8,128)} %param.20) | copy-start | bytes 30724
  10.8 11.7 %copy-start.7 = (s32[512]{0:T(512)S(1)}, s32[512]{0:T(512)}, u32[]{:S(2)}) copy-start(s32[512]{0:T(512)} %param.21) | copy-start | bytes 6148
  10.9 12.5 %copy-start.8 = (s32[512]{0:T(512)S(1)}, s32[512]{0:T(512)}, u32[]{:S(2)}) copy-start(s32[512]{0:T(512)} %param.22) | copy-start | bytes 6148
  411.3 4.0 copy-start.3
  414.0 2.7 copy-start.4
  415.3 6.1 %copy-start.2 = (f32[96,2,8,128]{3,1,2,0:T(2,128)S(1)}, f32[96,2,8,128]{3,1,2,0:T(2,128)}, u32[]{:S(2)}) copy-start(f32[96,2,8,128]{3,1,2,0:T(2,128)} %copy.25) | copy-start | bytes 2359300
Sparse Core Ops, SparseCore 0:
  9.8 42.5 all-gather.1
  448.8 54.9 all-reduce.4

commit v2 on v1

--- a/solution.py
+++ b/solution.py
@@ -45,112 +45,127 @@
     return pltpu.CompilerParams(dimension_semantics=sem, vmem_limit_bytes=vmem)
 
 
-def emit_codes(ids, mask, shift, out_ref):
-    n = ids.shape[1]
-    node = lax.broadcasted_iota(jnp.int32, (16, n), 1)
-    lo = (ids & 255).astype(F32)
-    code = jnp.where(mask > 0, (ids >> 8) * 16 + (node & 15) - shift, -384).astype(F32)
+def emit_codes(lo, hi, mask, shift, low_ref, high_ref, count_ref):
+    n = lo.shape[1]
+    node = (lax.broadcasted_iota(jnp.int32, (16, n), 1) & 15).astype(F32)
+    code = jnp.where(mask > 0, hi * 16.0 + node - shift, -384.0)
     count = jnp.maximum(jnp.sum(mask, axis=0, keepdims=True), 1).astype(F32)
-    count = jnp.broadcast_to(count, (16, n))
+    mine = (lax.broadcasted_iota(jnp.int32, (8, 128), 1) >> 4) == lax.broadcasted_iota(jnp.int32, (8, 128), 0)
+    fold = ((lax.broadcasted_iota(jnp.int32, (128, 256), 0) & 15)
+            == (lax.broadcasted_iota(jnp.int32, (128, 256), 1) & 15)).astype(F32).astype(BF16)
+    part = lax.broadcasted_iota(jnp.int32, (8, 256), 1) >> 4
     for c in range(n // 128):
         lanes = slice(c * 128, (c + 1) * 128)
-        stack = jnp.concatenate([lo[:, lanes], code[:, lanes], count[:, lanes],
-                                 jnp.zeros((80, 128), F32)], axis=0)
-        out_ref[lanes, :] = stack.T.astype(BF16)
+        count_ref[lanes, :] = jnp.broadcast_to(count[:, lanes], (128, 128)).T
+        for value, ref in ((lo, low_ref), (code, high_ref)):
+            spread = jnp.concatenate([jnp.where(mine, jnp.broadcast_to(value[k:k + 1, lanes], (8, 128)), 0.0)
+                                      for k in range(16)], axis=0)
+            folded = jnp.dot(spread.astype(BF16), fold, preferred_element_type=F32)
+            rows = folded[0:8, :]
+            for k in range(1, 16):
+                rows = jnp.where(part == k, folded[k * 8:k * 8 + 8, :], rows)
+            ref[c * 8:c * 8 + 8, :] = rows
 
 
 def pad_rows(x, rows):
     return jnp.concatenate([x, jnp.zeros((rows - x.shape[0], x.shape[1]), x.dtype)], axis=0)
 
 
-def compose_kernel(front_ref, nbr_ref, mask_ref, out_ref, table_ref):
-    n = nbr_ref.shape[1]
-    half = front_ref.shape[0] // 2
+def compose_kernel(front_ref, nbr_ref, mask_ref, low_ref, high_ref, count_ref, table_ref):
+    fan, n = nbr_ref.shape
 
     @pl.when(pl.program_id(0) == 0)
     def _():
-        table_ref[...] = front_ref[0:half, :] + (front_ref[half:2 * half, :] << 12)
-
-    nbr = pad_rows(nbr_ref[...], 16)
-    mask = pad_rows(mask_ref[...], 16)
-    tiles = [(s, c) for s in range(2) for c in range(n // 128)]
-    parts = [nbr[s * 8:s * 8 + 8, c * 128:c * 128 + 128] for s, c in tiles]
-    lane = [part & 127 for part in parts]
-    row = [part >> 7 for part in parts]
-    low = [r & (half - 1) for r in row]
-
-    def step(base, accs):
-        accs = list(accs)
-        block = table_ref[pl.ds(pl.multiple_of(base * 8, 8), 8), :]
-        for u in range(8):
-            entry = jnp.broadcast_to(block[u:u + 1, :], (8, 128))
-            at = base * 8 + u
-            for t in range(len(tiles)):
-                got = jnp.take_along_axis(entry, lane[t], axis=1, mode="promise_in_bounds")
-                accs[t] = jnp.where(low[t] == at, got, accs[t])
-        return tuple(accs)
-
-    accs = lax.fori_loop(0, half // 8, step, tuple(jnp.zeros((8, 128), jnp.int32) for _ in tiles))
-    ids = [jnp.where(row[t] >= half, accs[t] >> 12, accs[t]) & 4095 for t in range(len(tiles))]
-    cols = n // 128
-    ids = jnp.concatenate([jnp.concatenate(ids[s * cols:(s + 1) * cols], axis=1) for s in range(2)], axis=0)
-    emit_codes(ids, mask, 0, out_ref)
-
-
-def codes_kernel(shift, nbr_ref, mask_ref, out_ref):
-    emit_codes(pad_rows(nbr_ref[...], 16), pad_rows(mask_ref[...], 16), shift, out_ref)
+        ids = front_ref[...]
+        table_ref[0:128, :] = (ids & 255).astype(F32).T.astype(BF16)
+        table_ref[128:256, :] = (ids >> 8).astype(F32).T.astype(BF16)
+
+    row = lax.broadcasted_iota(jnp.int32, (256, n), 0).astype(F32).astype(BF16)
+    one = jnp.ones((16, n), BF16)
+    zero = jnp.zeros((16, n), BF16)
+    sub = lax.broadcasted_iota(jnp.int32, (8, n), 0)
+    lows, highs = [], []
+    for k in range(fan):
+        nbr = nbr_ref[k:k + 1, :]
+        want = jnp.broadcast_to((nbr >> 7).astype(F32), (16, n)).astype(BF16)
+        pick = jnp.concatenate([jnp.where(row[p * 16:p * 16 + 16, :] == want, one, zero) for p in range(16)], axis=0)
+        cand = jnp.dot(table_ref[...], pick, preferred_element_type=F32)
+        lane = jnp.broadcast_to(nbr & 127, (8, n))
+        low = jnp.zeros((8, n), F32)
+        high = jnp.zeros((8, n), F32)
+        for p in range(16):
+            hit = sub + p * 8 == lane
+            low = jnp.where(hit, cand[p * 8:p * 8 + 8, :], low)
+            high = jnp.where(hit, cand[128 + p * 8:136 + p * 8, :], high)
+        lows.append(jnp.sum(low, axis=0, keepdims=True))
+        highs.append(jnp.sum(high, axis=0, keepdims=True))
+    fill = [jnp.zeros((1, n), F32)] * (16 - fan)
+    emit_codes(jnp.concatenate(lows + fill, axis=0), jnp.concatenate(highs + fill, axis=0),
+               pad_rows(mask_ref[...], 16), 0.0, low_ref, high_ref, count_ref)
+
+
+def codes_kernel(shift, nbr_ref, mask_ref, low_ref, high_ref, count_ref):
+    ids = pad_rows(nbr_ref[...], 16)
+    emit_codes((ids & 255).astype(F32), (ids >> 8).astype(F32), pad_rows(mask_ref[...], 16), shift,
+               low_ref, high_ref, count_ref)
+
+
+def code_outs(n, block):
+    rows = pl.BlockSpec((block // 16, 256), lambda i: (i, 0))
+    shape = jax.ShapeDtypeStruct((n // 16, 256), F32)
+    return dict(out_specs=[rows, rows, pl.BlockSpec((block, 128), lambda i: (i, 0))],
+                out_shape=[shape, shape, jax.ShapeDtypeStruct((n, 128), F32)])
 
 
 def compose(frontier, nbr_t, mask_t, block=512):
-    n = nbr_t.shape[1]
+    fan, n = nbr_t.shape
     rows = frontier.shape[0] // 128
     return pl.pallas_call(
         compose_kernel,
         grid=(n // block,),
         in_specs=[pl.BlockSpec((rows, 128), lambda i: (0, 0)),
-                  pl.BlockSpec((nbr_t.shape[0], block), lambda i: (0, i)),
-                  pl.BlockSpec((nbr_t.shape[0], block), lambda i: (0, i))],
-        out_specs=pl.BlockSpec((block, 128), lambda i: (i, 0)),
-        out_shape=jax.ShapeDtypeStruct((n, 128), BF16),
-        scratch_shapes=[pltpu.VMEM((rows // 2, 128), jnp.int32)],
+                  pl.BlockSpec((fan, block), lambda i: (0, i)),
+                  pl.BlockSpec((fan, block), lambda i: (0, i))],
+        **code_outs(n, block),
+        scratch_shapes=[pltpu.VMEM((256, rows), BF16)],
         compiler_params=params_of("arbitrary"),
-        cost_estimate=pl.CostEstimate(flops=10**9, bytes_accessed=10**7, transcendentals=0),
+        cost_estimate=pl.CostEstimate(flops=2 * 65536 * fan * n, bytes_accessed=10**7, transcendentals=0),
         name="compose_ids",
     )(frontier.reshape(rows, 128), nbr_t, mask_t)
 
 
 def codes(nbr_t, mask_t, shift, block=512):
-    n = nbr_t.shape[1]
+    fan, n = nbr_t.shape
     return pl.pallas_call(
         functools.partial(codes_kernel, shift),
         grid=(n // block,),
-        in_specs=[pl.BlockSpec((nbr_t.shape[0], block), lambda i: (0, i)),
-                  pl.BlockSpec((nbr_t.shape[0], block), lambda i: (0, i))],
-        out_specs=pl.BlockSpec((block, 128), lambda i: (i, 0)),
-        out_shape=jax.ShapeDtypeStruct((n, 128), BF16),
+        in_specs=[pl.BlockSpec((fan, block), lambda i: (0, i)),
+                  pl.BlockSpec((fan, block), lambda i: (0, i))],
+        **code_outs(n, block),
         compiler_params=params_of("arbitrary"),
         name="codes",
     )(nbr_t, mask_t)
 
 
-def count_kernel(fan, halves, unroll, codes_ref, out_ref):
-    nodes = codes_ref.shape[0]
-    lane = lax.broadcasted_iota(jnp.int32, (16, 256), 1).astype(F32).astype(BF16)
+def count_kernel(halves, unroll, low_ref, high_ref, out_ref):
+    nodes = out_ref.shape[0]
+    row = lax.broadcasted_iota(jnp.int32, (256, 256), 0).astype(F32).astype(BF16)
     one = jnp.ones((16, 256), BF16)
     zero = jnp.zeros((16, 256), BF16)
 
+    def one_hot(want, less):
+        return [jnp.where(row[p * 16:p * 16 + 16, :] - less == want, one, zero) for p in range(16)]
+
     def group(g):
         at = pl.multiple_of(g * 16, 16)
-        block = codes_ref[pl.ds(at, 16), :]
-        low = [jnp.where(lane == block[:, k:k + 1], one, zero) for k in range(fan)]
-        low = jnp.concatenate(low + [zero] * (16 - fan), axis=0)
+        low = jnp.concatenate(one_hot(jnp.broadcast_to(low_ref[pl.ds(g, 1), :], (16, 256)).astype(BF16), 0), axis=0)
+        want = jnp.broadcast_to(high_ref[pl.ds(g, 1), :], (16, 256)).astype(BF16)
+        high = []
         for h in range(halves):
-            want = lane if h == halves - 1 else lane - 256
-            high = [jnp.where(want == block[:, 16 + k:17 + k], one, zero) for k in range(fan)]
-            high = jnp.concatenate(high + [zero] * (16 - fan), axis=0)
-            got = lax.dot_general(high, low, (((0,), (0,)), ((), ())), preferred_element_type=F32).astype(BF16)
-            for p in range(16):
-                out_ref[pl.ds(at, 16), (h * 16 + p) * 256:(h * 16 + p + 1) * 256] = got[p * 16:p * 16 + 16, :]
+            high += one_hot(want, 0 if h == halves - 1 else 256)
+        got = dot_t(jnp.concatenate(high, axis=0), low).astype(BF16)
+        for p in range(16 * halves):
+            out_ref[pl.ds(at, 16), p * 256:(p + 1) * 256] = got[p * 16:p * 16 + 16, :]
 
     def step(s, carry):
         for u in range(unroll):
@@ -160,18 +175,20 @@
     lax.fori_loop(0, nodes // (16 * unroll), step, 0)
 
 
-def count_matrix(code, fan, vocab, block=256, unroll=4):
-    n = code.shape[0]
-    return pl.pallas_call(
-        functools.partial(count_kernel, fan, vocab // 4096, unroll),
+def count_matrix(code, vocab, block=256, unroll=16):
+    low, high, _ = code
+    n = low.shape[0] * 16
+    rows = pl.BlockSpec((block // 16, 256), lambda i: (i, 0))
+    return pl.pallas_call(
+        functools.partial(count_kernel, vocab // 4096, unroll),
         grid=(n // block,),
-        in_specs=[pl.BlockSpec((block, 128), lambda i: (i, 0))],
+        in_specs=[rows, rows],
         out_specs=pl.BlockSpec((block, vocab), lambda i: (i, 0)),
         out_shape=jax.ShapeDtypeStruct((n, vocab), BF16),
         compiler_params=params_of("arbitrary"),
         cost_estimate=pl.CostEstimate(flops=2 * n * vocab * 256, bytes_accessed=2 * n * vocab, transcendentals=0),
         name="count_matrix",
-    )(code)
+    )(low, high)
 
 
 def norm_rows(z, gain, shift):
@@ -221,7 +238,7 @@
     lax.fori_loop(0, block // 32, fetch, 0)
     for c in range(tiles):
         hs_ref[:, c * 128:(c + 1) * 128] = got_ref[pl.ds(c, block, stride=8), :].astype(BF16)
-    count = codes_ref[:, 32:33].astype(F32)
+    count = codes_ref[:, 0:1]
     for c in range(feat // 256):
         cols = slice(c * 256, (c + 1) * 256)
         acc = jnp.dot(m_ref[...], x_ref[:, cols], preferred_element_type=F32)
@@ -264,7 +281,7 @@
 
 
 def layer_two_kernel(m_ref, codes_ref, h_all_ref, h_self_ref, w_self_ref, w_nbr_ref, vec_ref, a_ref, h_ref, z_ref):
-    count = codes_ref[:, 32:33].astype(F32)
+    count = codes_ref[:, 0:1]
     acc = jnp.dot(m_ref[...], h_all_ref[...], preferred_element_type=F32)
     a_ref[...] = (acc / count).astype(BF16)
     z = (jnp.dot(h_self_ref[...], w_self_ref[...], preferred_element_type=F32)
@@ -305,9 +322,20 @@
     return lax.dot_general(lhs, rhs, (((1,), (1,)), ((), ())), preferred_element_type=F32)
 
 
+def put_rows(ref, at, mat):
+    n = mat.shape[0]
+    ref[pl.ds(at, n, stride=2), :] = mat[:, 0:128]
+    ref[pl.ds(at + 1, n, stride=2), :] = mat[:, 128:256]
+
+
+def put_vector(ref, at, row):
+    ref[at:at + 1, :] = row[:, 0:128]
+    ref[at + 1:at + 2, :] = row[:, 128:256]
+
+
 def top_kernel(classes, nbr3_ref, mask3_ref, label_ref, valid_ref, h2_ref, a2_ref, z2_ref, h1_ref, codes2_ref,
                w3s_ref, w3n_ref, w2s_ref, w2n_ref, vec_ref,
-               g3s_ref, g3n_ref, g2s_ref, g2n_ref, vout_ref, dself_ref, dagg_ref, m3_ref, dh2_ref):
+               g3s_ref, g3n_ref, rows_ref, vout_ref, dself_ref, dagg_ref, m3_ref, dh2_ref):
     seeds = nbr3_ref.shape[0]
     n_two = h2_ref.shape[0]
     fan = nbr3_ref.shape[1]
@@ -345,18 +373,18 @@
     dh2_ref[0:seeds, :] += d_self3
     d_h2 = dh2_ref[...]
     d_z2, gain_terms = norm_back(z2_ref[...], vec_ref[1:2, :], d_h2, -1)
-    vout_ref[0:1, :] = jnp.sum(d_z2, axis=0, keepdims=True)
-    vout_ref[1:2, :] = jnp.sum(gain_terms, axis=0, keepdims=True)
-    vout_ref[2:3, :] = jnp.sum(d_h2, axis=0, keepdims=True)
-    vout_ref[3:4, :] = jnp.sum(d_logits, axis=0, keepdims=True)
-    vout_ref[4:5, :] = jnp.broadcast_to(loss, (1, HIDDEN))
-    vout_ref[5:6, :] = jnp.broadcast_to(n_valid, (1, HIDDEN))
-    vout_ref[6:8, :] = jnp.zeros((2, HIDDEN), F32)
+    vout_ref[0:1, :] = jnp.sum(d_logits, axis=0, keepdims=True)
+    vout_ref[1:2, :] = jnp.broadcast_to(loss, (1, HIDDEN))
+    vout_ref[2:3, :] = jnp.broadcast_to(n_valid, (1, HIDDEN))
+    vout_ref[3:8, :] = jnp.zeros((5, HIDDEN), F32)
     d_z2b = d_z2.astype(BF16)
-    g2s_ref[...] = tdot(h1_ref[...], d_z2b)
-    g2n_ref[...] = tdot(a2_ref[...], d_z2b)
+    put_rows(rows_ref, 0, tdot(h1_ref[...], d_z2b))
+    put_rows(rows_ref, 2 * HIDDEN, tdot(a2_ref[...], d_z2b))
+    for index, term in enumerate((d_z2, gain_terms, d_h2)):
+        put_vector(rows_ref, 4 * HIDDEN + 2 * index, jnp.sum(term, axis=0, keepdims=True))
+    rows_ref[4 * HIDDEN + 6:4 * HIDDEN + 8, :] = jnp.zeros((2, 128), F32)
     dself_ref[...] = dot_t(d_z2b, w2s_ref[...]).T
-    count2 = codes2_ref[:, 32:33].astype(F32)
+    count2 = codes2_ref[:, 0:1]
     dagg_ref[...] = (dot_t(d_z2b, w2n_ref[...]) / count2).T.astype(BF16)
 
 
@@ -364,9 +392,10 @@
     n_two = h2.shape[0]
     seeds = nbr3.shape[0]
     square = jax.ShapeDtypeStruct((HIDDEN, HIDDEN), F32)
+    rows = jax.ShapeDtypeStruct((4 * HIDDEN + 8, 128), F32)
     full = lambda x: pl.BlockSpec(x.shape, lambda i: (0, 0))
     args = (nbr3, mask3, label, valid, h2, a2, z2, h1, codes2, w3s, w3n, w2s, w2n, vecs)
-    outs = [square, square, square, square, jax.ShapeDtypeStruct((8, HIDDEN), F32),
+    outs = [square, square, rows, jax.ShapeDtypeStruct((8, HIDDEN), F32),
             jax.ShapeDtypeStruct((HIDDEN, n_two), F32), jax.ShapeDtypeStruct((HIDDEN, n_two), BF16)]
     specs = [full(x) for x in args]
     specs[7] = pl.BlockSpec((n_two, HIDDEN), lambda i: (0, 0))
@@ -382,17 +411,17 @@
     )(*args)
 
 
-def bottom_kernel(dagg_ref, m_ref, dself_ref, zt_ref, hs_ref, a_ref, gain_ref,
-                  gs_ref, gn_ref, vout_ref):
+def bottom_kernel(dagg_ref, m_ref, dself_ref, zt_ref, hs_ref, a_ref, gain_ref, rows_ref, gs_ref, gn_ref, vec_ref):
     pid = pl.program_id(0)
     block = m_ref.shape[1]
+    feat = hs_ref.shape[1]
     n_self = dself_ref.shape[1] // block
 
     @pl.when(pid == 0)
     def _():
         gs_ref[...] = jnp.zeros_like(gs_ref)
         gn_ref[...] = jnp.zeros_like(gn_ref)
-        vout_ref[...] = jnp.zeros_like(vout_ref)
+        vec_ref[...] = jnp.zeros_like(vec_ref)
 
     d_h = jnp.dot(dagg_ref[...], m_ref[...], preferred_element_type=F32)
     at = pl.multiple_of(jnp.minimum(pid, n_self - 1) * block, block)
@@ -400,17 +429,26 @@
     d_z, gain_terms = norm_back(zt_ref[...], gain_ref[:, 0:1], d_h, 0)
     sums = [jnp.sum(term, axis=1, keepdims=True) for term in (d_z, gain_terms, d_h)]
     lane = lax.broadcasted_iota(jnp.int32, (HIDDEN, 128), 1)
-    vout_ref[...] += jnp.where(lane == 0, sums[0], jnp.where(lane == 1, sums[1], jnp.where(lane == 2, sums[2], 0.0)))
+    vec_ref[...] += jnp.where(lane == 0, sums[0], jnp.where(lane == 1, sums[1], jnp.where(lane == 2, sums[2], 0.0)))
     d_zb = d_z.astype(BF16)
     gs_ref[...] += jnp.dot(d_zb, hs_ref[...], preferred_element_type=F32)
     gn_ref[...] += jnp.dot(d_zb, a_ref[...], preferred_element_type=F32)
+
+    @pl.when(pid == pl.num_programs(0) - 1)
+    def _():
+        put_rows(rows_ref, 0, gs_ref[...].T)
+        put_rows(rows_ref, 2 * feat, gn_ref[...].T)
+        vectors = vec_ref[...].T
+        for index in range(3):
+            put_vector(rows_ref, 4 * feat + 2 * index, vectors[index:index + 1, :])
+        rows_ref[4 * feat + 6:4 * feat + 8, :] = jnp.zeros((2, 128), F32)
 
 
 def bottom(dagg_t, m_two, dself_t, z_t, h_self, a_one, gain_col, block=512):
     n_two, n = m_two.shape
     feat = h_self.shape[1]
     whole = lambda i: (0, 0)
-    grads = jax.ShapeDtypeStruct((HIDDEN, feat), F32)
+    rows = 4 * feat + 8
     return pl.pallas_call(
         bottom_kernel,
         grid=(n // block,),
@@ -421,13 +459,112 @@
                   pl.BlockSpec((block, feat), lambda i: (i, 0)),
                   pl.BlockSpec((block, feat), lambda i: (i, 0)),
                   pl.BlockSpec((HIDDEN, 128), whole)],
-        out_specs=[pl.BlockSpec((HIDDEN, feat), whole), pl.BlockSpec((HIDDEN, feat), whole),
-                   pl.BlockSpec((HIDDEN, 128), whole)],
-        out_shape=[grads, grads, jax.ShapeDtypeStruct((HIDDEN, 128), F32)],
+        out_specs=pl.BlockSpec((rows, 128), whole),
+        out_shape=jax.ShapeDtypeStruct((rows, 128), F32),
+        scratch_shapes=[pltpu.VMEM((HIDDEN, feat), F32), pltpu.VMEM((HIDDEN, feat), F32), pltpu.VMEM((HIDDEN, 128), F32)],
         compiler_params=params_of("arbitrary"),
         cost_estimate=pl.CostEstimate(flops=2 * n * n_two * HIDDEN, bytes_accessed=2 * n * n_two, transcendentals=0),
         name="layer_one_back",
     )(dagg_t, m_two, dself_t, z_t, h_self, a_one, gain_col)
+
+
+CHUNKS = 4
+
+
+def sum_kernel(low_ref, mid_ref, top_ref, out_ref, buf_ref, in0_ref, in1_ref, in2_ref, send_sem, recv_sem):
+    me = lax.axis_index('dp')
+    core = me % 2
+    x_bit = (me // 2) % 2
+    y_bit = me // 4
+    x_peer = me + 2 - 4 * x_bit
+    y_peer = me + 4 - 8 * y_bit
+    mate = me + 1 - 2 * core
+    first = x_bit + core * (y_bit - x_bit)
+    second = y_bit + core * (x_bit - y_bit)
+    peer_one = x_peer + core * (y_peer - x_peer)
+    peer_two = y_peer + core * (x_peer - y_peer)
+    barrier = pltpu.get_barrier_semaphore()
+    for peer in (mate, x_peer, y_peer):
+        pl.semaphore_signal(barrier, inc=1, device_id=(peer,), device_id_type=pl.DeviceIdType.MESH)
+    n_low = low_ref.shape[0] - 2
+    n_mid = mid_ref.shape[0] - 2
+    n_top = top_ref.shape[0]
+    buf_ref[0:n_low, :] = low_ref[0:n_low, :]
+    buf_ref[n_low:n_low + n_mid, :] = mid_ref[0:n_mid, :]
+    buf_ref[n_low + n_mid:n_low + n_mid + n_top, :] = top_ref[...]
+    pl.semaphore_wait(barrier, 3)
+
+    size = buf_ref.shape[0] // CHUNKS
+    half, quarter, eighth = size // 2, size // 4, size // 8
+
+    def rows(ref, at, count):
+        return ref.at[pl.ds(pl.multiple_of(at, 8), count), :]
+
+    def copy(chunk, phase):
+        base = chunk * size + core * half
+        if phase == 0:
+            src, dst, peer = rows(buf_ref, chunk * size + (1 - core) * half, half), in0_ref.at[chunk], mate
+        elif phase == 1:
+            src, dst, peer = rows(buf_ref, base + (1 - first) * quarter, quarter), in1_ref.at[chunk], peer_one
+        elif phase == 2:
+            at = base + first * quarter + (1 - second) * eighth
+            src, dst, peer = rows(buf_ref, at, eighth), in2_ref.at[chunk], peer_two
+        elif phase == 3:
+            at = base + first * quarter + second * eighth
+            src, dst, peer = rows(out_ref, at, eighth), rows(out_ref, at, eighth), peer_two
+        elif phase == 4:
+            at = base + first * quarter
+            src, dst, peer = rows(out_ref, at, quarter), rows(out_ref, at, quarter), peer_one
+        else:
+            src, dst, peer = rows(out_ref, base, half), rows(out_ref, base, half), mate
+        return pltpu.make_async_remote_copy(
+            src_ref=src, dst_ref=dst, send_sem=send_sem.at[chunk, phase], recv_sem=recv_sem.at[chunk, phase],
+            device_id=(peer,), device_id_type=pl.DeviceIdType.MESH)
+
+    def absorb(chunk, phase):
+        base = chunk * size + core * half
+        if phase == 0:
+            at = pl.ds(pl.multiple_of(base, 8), half)
+            buf_ref[at, :] = buf_ref[at, :] + in0_ref[chunk]
+        elif phase == 1:
+            at = pl.ds(pl.multiple_of(base + first * quarter, 8), quarter)
+            buf_ref[at, :] = buf_ref[at, :] + in1_ref[chunk]
+        elif phase == 2:
+            at = pl.ds(pl.multiple_of(base + first * quarter + second * eighth, 8), eighth)
+            out_ref[at, :] = buf_ref[at, :] + in2_ref[chunk]
+
+    copies = {}
+    for tick in range(6 + CHUNKS):
+        for chunk in range(CHUNKS):
+            phase = tick - chunk
+            if phase >= 1 and phase <= 6:
+                copies[chunk, phase - 1].wait_recv()
+                absorb(chunk, phase - 1)
+            if phase >= 0 and phase <= 5:
+                copies[chunk, phase] = copy(chunk, phase)
+                copies[chunk, phase].start()
+    for done in copies.values():
+        done.wait_send()
+
+
+def sum_devices(low, mid, top_rows):
+    n = low.shape[0] + mid.shape[0] + top_rows.shape[0] - 4
+    vmem = pl.BlockSpec(memory_space=pltpu.VMEM)
+    size = n // CHUNKS
+    return pl.pallas_call(
+        sum_kernel,
+        in_specs=[vmem] * 3,
+        out_specs=vmem,
+        out_shape=jax.ShapeDtypeStruct((n, 128), F32),
+        scratch_shapes=[pltpu.VMEM((n, 128), F32),
+                        pltpu.VMEM((CHUNKS, size // 2, 128), F32),
+                        pltpu.VMEM((CHUNKS, size // 4, 128), F32),
+                        pltpu.VMEM((CHUNKS, size // 8, 128), F32),
+                        pltpu.SemaphoreType.DMA((CHUNKS, 6)),
+                        pltpu.SemaphoreType.DMA((CHUNKS, 6))],
+        compiler_params=pltpu.CompilerParams(collective_id=1, has_side_effects=True, vmem_limit_bytes=VMEM_ALL),
+        name="sum_devices",
+    )(low, mid, top_rows)
 
 
 def adam_update(params, adam_m, adam_v, grads):
@@ -456,29 +593,31 @@
         w3s = jnp.pad(pieces[10], pad3).astype(BF16)
         w3n = jnp.pad(pieces[11], pad3).astype(BF16)
         code_one = compose(frontier, nbr_l1.T, mask_l1.T)
-        code_two = codes(nbr_l2.T, mask_l2.T, 256)
-        m_one = count_matrix(code_one, nbr_l1.shape[1], table.shape[0])
-        m_two = count_matrix(code_two, nbr_l2.shape[1], n_one)
+        code_two = codes(nbr_l2.T, mask_l2.T, 256.0)
+        m_one = count_matrix(code_one, table.shape[0])
+        m_two = count_matrix(code_two, n_one)
         h_self, a_one, h_one, z_one_t = layer_one(
-            m_one, code_one, table, frontier[:n_one], pieces[0].astype(BF16), pieces[1].astype(BF16),
+            m_one, code_one[2], table, frontier[:n_one], pieces[0].astype(BF16), pieces[1].astype(BF16),
             stack_rows(pieces[2], pieces[3], pieces[4]))
-        a_two, h_two, z_two = layer_two(m_two, code_two, h_one, pieces[5].astype(BF16), pieces[6].astype(BF16),
+        a_two, h_two, z_two = layer_two(m_two, code_two[2], h_one, pieces[5].astype(BF16), pieces[6].astype(BF16),
                                         stack_rows(pieces[7], pieces[8], pieces[9]))
-        g3s, g3n, g2s, g2n, vout, dself_t, dagg_t = top(
-            classes, nbr_l3, mask_l3, labels[:, None], seed_mask[:, None], h_two, a_two, z_two, h_one, code_two,
+        g3s, g3n, mid_rows, vout, dself_t, dagg_t = top(
+            classes, nbr_l3, mask_l3, labels[:, None], seed_mask[:, None], h_two, a_two, z_two, h_one, code_two[2],
             w3s, w3n, pieces[5].astype(BF16), pieces[6].astype(BF16),
             stack_rows(pieces[7], pieces[8], pieces[9], pieces[12]))
         gain_col = jnp.broadcast_to(pieces[3][:, None], (HIDDEN, 128))
-        g1s, g1n, vone = bottom(dagg_t, m_two, dself_t, z_one_t, h_self, a_one, gain_col)
-        sums = jnp.concatenate([
-            g1s.T.reshape(-1), g1n.T.reshape(-1), vone[:, 0], vone[:, 1], vone[:, 2],
-            g2s.reshape(-1), g2n.reshape(-1), vout[0], vout[1], vout[2],
-            g3s[:, :classes].reshape(-1), g3n[:, :classes].reshape(-1), vout[3, :classes],
-            vout[4, :1], vout[5, :1]])
-        sums = lax.psum(sums, 'dp')
-        total = jnp.maximum(sums[-1], 1.0)
-        loss = sums[-2] / total
-        return (loss,) + adam_update(params, adam_m, adam_v, sums[:-2] / total)
+        low_rows = bottom(dagg_t, m_two, dself_t, z_one_t, h_self, a_one, gain_col)
+        n_params = params.shape[0]
+        done = (low_rows.shape[0] + mid_rows.shape[0] - 4) * 128
+        unit = 64 * CHUNKS * 128
+        whole = -(-(n_params + 2) // unit) * unit
+        top_rows = jnp.concatenate([g3s[:, :classes].reshape(-1), g3n[:, :classes].reshape(-1), vout[0, :classes],
+                                    vout[1, :1], vout[2, :1],
+                                    jnp.zeros((whole - n_params - 2,), F32)]).reshape((whole - done) // 128, 128)
+        sums = sum_devices(low_rows, mid_rows, top_rows).reshape(-1)
+        total = jnp.maximum(sums[n_params + 1], 1.0)
+        loss = sums[n_params] / total
+        return (loss,) + adam_update(params, adam_m, adam_v, sums[:n_params] / total)
 
     row_spec = P('dp')
     replicated = P()

time: 523 us -> 349 us (0.67)
  Pallas kernels: 381 us -> 293 us
  waiting for transfers between devices: 55.8 us -> 0.68 us
  local copies, waits for them, and re-layouts: 58.6 us -> 28.8 us
    psum x1 -> x0, waiting for transfers between devices: 55.1 us -> none  [body(): sums = lax.psum(sums, 'dp')]
    pallas_call x2 -> x3, Pallas kernels: 146 us -> 93.8 us  [the longest x2 50.3 us: count_matrix(): pl.pallas_call(functools.partial(count_kernel, vocab // 4096, unroll), gr...]
    pallas_call x1, Pallas kernels: 66.7 us -> 29.5 us  [compose(): pl.pallas_call(compose_kernel, grid=(n // block,), in_specs=[pl.BlockSpec...]
    concatenate x1, local copies, waits for them, and re-layouts: 27.2 us -> 7.13 us  [body(): jnp.concatenate([g3s[:, :classes].reshape(-1), g3n[:, :classes].reshape(-...]
  transfers between devices with their start and end apart: 2 -> 1, of which waited for: 1 -> 0; matrix products, arithmetic and copies ran while one was open for 3% -> 5% of each run, Pallas kernels for 41% -> 24%
where the time goes in v2:
time: 349 us; the launch traced here: 348 us
  Pallas kernels  293 us (84%)
  local copies, waits for them, and re-layouts  28.8 us (8%)
  between operations  16.6 us (5%)
  other arithmetic  8.95 us (3%)
    pallas_call x1, Pallas kernels, layer_one(): pl.pallas_call(layer_one_kernel, grid_spec=pltpu.PrefetchScalarGridSpec(n...  98.2 us
    pallas_call x2, Pallas kernels, count_matrix(): pl.pallas_call(functools.partial(count_kernel, vocab // 4096, unroll), gr...  50.3 us
    pallas_call x1, Pallas kernels, sum_devices(): pl.pallas_call(sum_kernel, in_specs=[vmem] * 3, out_specs=vmem, out_shape...  43.5 us
    pallas_call x1, Pallas kernels, bottom(): pl.pallas_call(bottom_kernel, grid=(n // block,), in_specs=[pl.BlockSpec(...  34.3 us
    pallas_call x1, Pallas kernels, compose(): pl.pallas_call(compose_kernel, grid=(n // block,), in_specs=[pl.BlockSpec...  29.5 us
    pallas_call x1, Pallas kernels, layer_two(): pl.pallas_call(layer_two_kernel, grid=(n // block,), in_specs=[pl.BlockSp...  20.8 us
    pallas_call x1, Pallas kernels, top(): pl.pallas_call(functools.partial(top_kernel, classes), grid=(1,), in_spec...  12.5 us
    sub x1, other arithmetic, adam_update(): params - ADAM_LR * m_hat / (jnp.sqrt(v_hat) + ADAM_EPS)  7.15 us
  transfers between devices with their start and end apart: 1, of which 0 were waited for; matrix products, arithmetic and copies ran while one was open for 5% of the time, Pallas kernels for 24%

profile of v2, /device:TPU:0, one launch (start us, length us, event | category | flops | bytes accessed | tf_op | source)
XLA Modules:
  0.0 347.7 jit_solution(12863903751798313196)
XLA Ops:
  7.2 0.0 all-gather.2.cloned.1.call-start
  7.2 0.7 all-gather.2.cloned.1.call-update
  7.9 1.8 convert.14
  9.7 0.0 copy-start.1
  9.7 0.0 slice-start
  9.7 0.0 copy-start
  9.7 1.0 copy-done.1
  10.7 0.0 copy-start.2
  10.7 0.1 fusion.6
  10.8 0.0 copy-start.3
  10.8 0.0 copy-start.4
  10.8 0.0 copy-start.5
  10.8 0.9 convert_element_type.21.w_self_ref
  11.7 0.9 convert_element_type.22.w_nbr_ref
  12.6 1.4 slice.72.self_ids
  14.0 1.0 fusion.5
  15.0 0.7 convert_element_type.23.w_self_ref.w2s_ref
  15.7 0.7 convert_element_type.24.w_nbr_ref.w2n_ref
  16.4 0.0 slice-done
  16.4 0.0 copy-done
  16.5 0.6 stack.40.vec_ref
  17.1 0.6 stack.42.vec_ref
  17.7 1.0 fusion.4
  18.7 0.4 reshape.43
  19.1 0.4 reshape.44
  19.4 0.7 pad.13.w3s_ref
  20.1 0.7 pad.14.w3n_ref
  20.8 0.0 copy-done.2
  20.8 0.9 copy.19.nbr3_ref
  21.7 0.0 copy-done.3
  21.7 0.8 copy.20.mask3_ref
  22.5 0.0 copy-done.4
  22.5 0.9 copy.21.label_ref
  23.4 0.0 copy-done.5
  23.4 0.9 copy.22.valid_ref
  24.2 3.6 %codes.1 = (f32[128,256]{1,0:T(8,128)}, f32[128,256]{1,0:T(8,128)}, f32[2048,128]{1,0:T(8,128)}) custom-call(s32[10,2048]{1,0:T(8,128)} %bitcast.28, s32[10,2048]{1,0:T(8,128)} %bitcast.29), custom_call_target="tpu_custom_call" | custom-call | tf_op jit(solution)/shard_map/codes/pallas_call | solution.py:139
  27.8 0.6 stack.36.vec_ref
  28.4 15.2 %count_matrix.2.m_ref = bf16[2048,8192]{1,0:T(8,128)(2,1)} custom-call(f32[128,256]{1,0:T(8,128)} %get-tuple-element.23.low_ref, f32[128,256]{1,0:T(8,128)} %get-tuple-element.24.high_ref), custom_call_target="tpu_custom_call" | custom-call | flops 8589934592 | bytes 33554432 | tf_op jit(solution)/shard_map/count_matrix/pallas_call | solution.py:182
  43.6 29.5 %compose_ids.1 = (f32[512,256]{1,0:T(8,128)}, f32[512,256]{1,0:T(8,128)}, f32[8192,128]{1,0:T(8,128)}) custom-call(s32[256,128]{1,0:T(8,128)} %bitcast.37, s32[15,8192]{1,0:T(8,128)} %bitcast.44, s32[15,8192]{1,0:T(8,128)} %bitcast.45), custom_call_target="tpu_custom_call" | custom-call | flops 16106127360 | bytes 10000000 | tf_op jit(solution)/shard_map/compose_ids/pallas_call | solution.py:123
  73.1 35.1 %count_matrix.3.m_ref = bf16[8192,4096]{1,0:T(8,128)(2,1)} custom-call(f32[512,256]{1,0:T(8,128)} %get-tuple-element.26.low_ref, f32[512,256]{1,0:T(8,128)} %get-tuple-element.27.high_ref), custom_call_target="tpu_custom_call" | custom-call | flops 17179869184 | bytes 67108864 | tf_op jit(solution)/shard_map/count_matrix/pallas_call | solution.py:182
  108.2 0.0 all-gather.2.cloned.1.call-done.x_ref
  108.2 98.2 %layer_one.1 = (bf16[8192,768]{1,0:T(8,128)(2,1)}, bf16[8192,768]{1,0:T(8,128)(2,1)}, bf16[8192,256]{1,0:T(8,128)(2,1)}, f32[256,8192]{1,0:T(8,128)}) custom-call(s32[8192]{0:T(1024)} %slice.72.self_ids, bf16[8192,4096]{1,0:T(8,128)(2,1)} %count_matrix.3.m_ref, f32[8192,128]{1,0:T(8,128)} %get-tuple-element.28.codes_ref, ...), custom_call_target="tpu_custom_call" | custom-call | flops 51539607552 | bytes 67108864 | tf_op jit(solution)/shard_map/layer_one/pallas_call | solution.py:257
  206.4 20.8 %layer_two.1 = (bf16[2048,256]{1,0:T(8,128)(2,1)}, bf16[2048,256]{1,0:T(8,128)(2,1)}, f32[2048,256]{1,0:T(8,128)}) custom-call(bf16[2048,8192]{1,0:T(8,128)(2,1)} %count_matrix.2.m_ref, f32[2048,128]{1,0:T(8,128)} %get-tuple-element.25.codes_ref.codes2_ref, bf16[8192,256]{1,0:T(8,128)(2,1)} %get-tuple-element.29.h_all_ref.h_self_ref.h1_ref, ...), custom_call_target="tpu_custom_call" | custom-call | flops 8589934592 | bytes 33554432 | tf_op jit(solution)/shard_map/layer_two/pallas_call | solution.py:297
  227.2 12.5 %layer_three.1 = (f32[256,256]{1,0:T(8,128)}, f32[256,256]{1,0:T(8,128)}, f32[1032,128]{1,0:T(8,128)}, f32[8,256]{1,0:T(8,128)}, f32[256,2048]{1,0:T(8,128)}, /*index=5*/bf16[256,2048]{1,0:T(8,128)(2,1)}) custom-call(s32[512,5]{1,0:T(8,128)} %copy.19.nbr3_ref, s32[512,5]{1,0:T(8,128)} %copy.20.mask3_ref, s32[512,1]{1,0:T(8,128)} %copy.21.label_ref, ...), custom_call_target="tpu_custom_call" | custom-call | tf_op jit(solution)/shard_map/layer_three/pallas_call | solution.py:402
  239.7 1.3 fusion.7
  241.0 0.7 slice.88
  241.7 1.3 reshape.45
  243.0 1.3 reshape.46
  244.3 7.1 %concatenate.3 = f32[96768]{0:T(1024)} concatenate(f32[39168]{0:T(1024)S(1)} %reshape.45, f32[39168]{0:T(1024)S(1)} %reshape.46, f32[153]{0:T(256)S(1)} %bitcast.38, f32[1]{0:T(128)} %bitcast.15, f32[1]{0:T(128)} %bitcast.16, f32[18277]{0:T(1024)S(1)} %broadcast_in_dim.18), dimensions={0} | concatenate | bytes 774144 | tf_op jit(solution)/shard_map/concatenate | solution.py:614
  251.4 0.8 broadcast_in_dim.17.gain_ref
  252.2 34.3 %layer_one_back.1.low_ref = f32[3080,128]{1,0:T(8,128)} custom-call(bf16[256,2048]{1,0:T(8,128)(2,1)} %get-tuple-element.33.dagg_ref, bf16[2048,8192]{1,0:T(8,128)(2,1)} %count_matrix.2.m_ref, f32[256,2048]{1,0:T(8,128)} %get-tuple-element.34.dself_ref, f32[256,8192]{1,0:T(8,128)} %get-tuple-element.35.zt_ref, bf16[8192,768]{1,0:T(8,128)(2,1)} %get-tuple-element.36.hs_ref, ...), custom_call_target="tpu_custom_call" | custom-call | flops 8589934592 | bytes 33554432 | tf_op jit(solution)/shard_map/layer_one_back/pallas_call | solution.py:452
  286.4 43.5 %sum_devices.1 = f32[4864,128]{1,0:T(8,128)} custom-call(f32[3080,128]{1,0:T(8,128)} %layer_one_back.1.low_ref, f32[1032,128]{1,0:T(8,128)} %get-tuple-element.38.mid_ref, f32[756,128]{1,0:T(8,128)} %bitcast.25), custom_call_target="tpu_custom_call" | custom-call | tf_op jit(solution)/shard_map/sum_devices/pallas_call | solution.py:554
  330.0 1.3 fusion.2
  332.6 7.1 %divide_subtract_fusion = (f32[604313]{0:T(1024)}, f32[604313]{0:T(1024)}, f32[604313]{0:T(1024)}) fusion(f32[604313]{0:T(1024)S(1)} %copy-done, f32[]{:T(128)} %bitcast.20, f32[622592]{0:T(1024)} %bitcast.24, f32[604313]{0:T(1024)} %param.24, f32[604313]{0:T(1024)} %param.25), kind=kLoop, calls=%fused_computation.3 | loop fusion | flops 7856069 | bytes 16920768 | tf_op jit(solution)/shard_map/sub | solution.py:575
  (5 shorter events, 0.0 us)
Async XLA Ops:
  7.2 101.0 %all-gather.2.cloned.1.call-start = ((), (), s32[]{:S(2)}) async-start(), calls=%async_computation | async-start | bytes 7077888 | tf_op jit(solution)/shard_map/all_gather | solution.py:590
  9.7 1.0 copy-start.1
  9.7 6.7 %slice-start = ((f32[604313]{0:T(1024)}), f32[153]{0:T(256)S(1)}, s32[]{:S(2)}) async-start(f32[604313]{0:T(1024)} %param.23), calls=%async_computation.1 | async-start | bytes 2048 | tf_op jit(solution)/shard_map/slice | solution.py:39
  9.7 6.7 %copy-start = (f32[604313]{0:T(1024)S(1)}, f32[604313]{0:T(1024)}, u32[]{:S(2)}) copy-start(f32[604313]{0:T(1024)} %param.23) | copy-start | bytes 7251760
  10.7 10.1 %copy-start.2 = (s32[512,5]{0,1:T(8,128)S(1)}, s32[512,5]{0,1:T(8,128)}, u32[]{:S(2)}) copy-start(s32[512,5]{0,1:T(8,128)} %param.19) | copy-start | bytes 30724
  10.8 10.9 %copy-start.3 = (s32[512,5]{0,1:T(8,128)S(1)}, s32[512,5]{0,1:T(8,128)}, u32[]{:S(2)}) copy-start(s32[512,5]{0,1:T(8,128)} %param.20) | copy-start | bytes 30724
  10.8 11.7 %copy-start.4 = (s32[512]{0:T(512)S(1)}, s32[512]{0:T(512)}, u32[]{:S(2)}) copy-start(s32[512]{0:T(512)} %param.21) | copy-start | bytes 6148
  10.8 12.6 %copy-start.5 = (s32[512]{0:T(512)S(1)}, s32[512]{0:T(512)}, u32[]{:S(2)}) copy-start(s32[512]{0:T(512)} %param.22) | copy-start | bytes 6148
Sparse Core Ops, SparseCore 0:
  9.8 42.4 all-gather.1

commit v3 on v2

v3 whole, which is shorter than its diff:
```python
import functools

import jax
import jax.numpy as jnp
from jax import lax
from jax.experimental import pallas as pl
from jax.experimental.pallas import tpu as pltpu
from jax.sharding import PartitionSpec as P

HIDDEN = 256
LANES = 128
WIDE = 256
GROUP = 16
SUB = 8
STEP = 10
LN_EPS = 1e-5
BETA_ONE = 0.9
BETA_TWO = 0.999
ADAM_LR = 3e-3
ADAM_EPS = 1e-8
F32 = jnp.float32
BF16 = jnp.bfloat16
F8 = jnp.float8_e4m3fn
VMEM_ALL = 60 * 1024 * 1024


def class_count(n_params, feat):
    return (n_params - 2 * feat * HIDDEN - 6 * HIDDEN - 2 * HIDDEN * HIDDEN) // (2 * HIDDEN + 1)


def params_of(*sem, vmem=VMEM_ALL):
    return pltpu.CompilerParams(dimension_semantics=sem, vmem_limit_bytes=vmem)


def emit_codes(lo, hi, mask, shift, low_ref, high_ref, count_ref):
    n = lo.shape[1]
    node = (lax.broadcasted_iota(jnp.int32, (GROUP, n), 1) & 15).astype(F32)
    code = jnp.where(mask > 0, hi * 16.0 + node - shift, -384.0)
    count = jnp.maximum(jnp.sum(mask, axis=0, keepdims=True), 1).astype(F32)
    mine = (lax.broadcasted_iota(jnp.int32, (SUB, LANES), 1) >> 4) == lax.broadcasted_iota(jnp.int32, (SUB, LANES), 0)
    fold = ((lax.broadcasted_iota(jnp.int32, (LANES, WIDE), 0) & 15)
            == (lax.broadcasted_iota(jnp.int32, (LANES, WIDE), 1) & 15)).astype(F32).astype(BF16)
    part = lax.broadcasted_iota(jnp.int32, (SUB, WIDE), 1) >> 4
    for c in range(n // LANES):
        lanes = slice(c * LANES, (c + 1) * LANES)
        count_ref[lanes, :] = jnp.broadcast_to(count[:, lanes], (LANES, LANES)).T
        for value, ref in ((lo, low_ref), (code, high_ref)):
            spread = jnp.concatenate([jnp.where(mine, jnp.broadcast_to(value[k:k + 1, lanes], (SUB, LANES)), 0.0)
                                      for k in range(GROUP)], axis=0)
            folded = jnp.dot(spread.astype(BF16), fold, preferred_element_type=F32)
            rows = folded[0:SUB, :]
            for k in range(1, GROUP):
                rows = jnp.where(part == k, folded[k * SUB:k * SUB + SUB, :], rows)
            ref[c * SUB:c * SUB + SUB, :] = rows


def pad_rows(x, rows):
    return jnp.concatenate([x, jnp.zeros((rows - x.shape[0], x.shape[1]), x.dtype)], axis=0)


def compose_kernel(front_ref, nbr_ref, mask_ref, low_ref, high_ref, count_ref, table_ref):
    fan, n = nbr_ref.shape

    @pl.when(pl.program_id(0) == 0)
    def _():
        ids = front_ref[...]
        table_ref[0:LANES, :] = (ids & 255).astype(F32).T.astype(BF16)
        table_ref[LANES:WIDE, :] = (ids >> SUB).astype(F32).T.astype(BF16)

    row = lax.broadcasted_iota(jnp.int32, (WIDE, n), 0).astype(F32).astype(BF16)
    one = jnp.ones((GROUP, n), BF16)
    zero = jnp.zeros((GROUP, n), BF16)
    sub = lax.broadcasted_iota(jnp.int32, (SUB, n), 0)
    lows, highs = [], []
    for k in range(fan):
        nbr = nbr_ref[k:k + 1, :]
        want = jnp.broadcast_to((nbr >> 7).astype(F32), (GROUP, n)).astype(BF16)
        pick = jnp.concatenate([jnp.where(row[p * GROUP:p * GROUP + GROUP, :] == want, one, zero) for p in range(GROUP)], axis=0)
        cand = jnp.dot(table_ref[...], pick, preferred_element_type=F32)
        lane = jnp.broadcast_to(nbr & 127, (SUB, n))
        low = jnp.zeros((SUB, n), F32)
        high = jnp.zeros((SUB, n), F32)
        for p in range(GROUP):
            hit = sub + p * SUB == lane
            low = jnp.where(hit, cand[p * SUB:p * SUB + SUB, :], low)
            high = jnp.where(hit, cand[LANES + p * SUB:136 + p * SUB, :], high)
        lows.append(jnp.sum(low, axis=0, keepdims=True))
        highs.append(jnp.sum(high, axis=0, keepdims=True))
    fill = [jnp.zeros((1, n), F32)] * (GROUP - fan)
    emit_codes(jnp.concatenate(lows + fill, axis=0), jnp.concatenate(highs + fill, axis=0),
               pad_rows(mask_ref[...], GROUP), 0.0, low_ref, high_ref, count_ref)


def codes_kernel(shift, nbr_ref, mask_ref, low_ref, high_ref, count_ref):
    ids = pad_rows(nbr_ref[...], GROUP)
    emit_codes((ids & 255).astype(F32), (ids >> SUB).astype(F32), pad_rows(mask_ref[...], GROUP), shift,
               low_ref, high_ref, count_ref)


def code_outs(n, block):
    rows = pl.BlockSpec((block // GROUP, WIDE), lambda i: (i, 0))
    shape = jax.ShapeDtypeStruct((n // GROUP, WIDE), F32)
    return dict(out_specs=[rows, rows, pl.BlockSpec((block, LANES), lambda i: (i, 0))],
                out_shape=[shape, shape, jax.ShapeDtypeStruct((n, LANES), F32)])


def compose(frontier, nbr_t, mask_t, block=512):
    fan, n = nbr_t.shape
    rows = frontier.shape[0] // LANES
    return pl.pallas_call(
        compose_kernel,
        grid=(n // block,),
        in_specs=[pl.BlockSpec((rows, LANES), lambda i: (0, 0)),
                  pl.BlockSpec((fan, block), lambda i: (0, i)),
                  pl.BlockSpec((fan, block), lambda i: (0, i))],
        **code_outs(n, block),
        scratch_shapes=[pltpu.VMEM((WIDE, rows), BF16)],
        compiler_params=params_of("arbitrary"),
        cost_estimate=pl.CostEstimate(flops=2 * 65536 * fan * n, bytes_accessed=10**7, transcendentals=0),
        name="compose_ids",
    )(frontier.reshape(rows, LANES), nbr_t, mask_t)


def codes(nbr_t, mask_t, shift, block=512):
    fan, n = nbr_t.shape
    return pl.pallas_call(
        functools.partial(codes_kernel, shift),
        grid=(n // block,),
        in_specs=[pl.BlockSpec((fan, block), lambda i: (0, i)),
                  pl.BlockSpec((fan, block), lambda i: (0, i))],
        **code_outs(n, block),
        compiler_params=params_of("arbitrary"),
        name="codes",
    )(nbr_t, mask_t)


def count_kernel(halves, unroll, low_ref, high_ref, out_ref):
    nodes = out_ref.shape[0]
    row = lax.broadcasted_iota(jnp.int32, (WIDE, WIDE), 0).astype(F32).astype(BF16)
    one = jnp.ones((GROUP, WIDE), BF16)
    zero = jnp.zeros((GROUP, WIDE), BF16)

    def one_hot(want, less):
        return [jnp.where(row[p * GROUP:p * GROUP + GROUP, :] - less == want, one, zero) for p in range(GROUP)]

    def group(g):
        at = pl.multiple_of(g * GROUP, GROUP)
        low = jnp.concatenate(one_hot(jnp.broadcast_to(low_ref[pl.ds(g, 1), :], (GROUP, WIDE)).astype(BF16), 0), axis=0)
        want = jnp.broadcast_to(high_ref[pl.ds(g, 1), :], (GROUP, WIDE)).astype(BF16)
        high = []
        for h in range(halves):
            high += one_hot(want, 0 if h == halves - 1 else WIDE)
        got = dot_t(jnp.concatenate(high, axis=0).astype(F8), low.astype(F8)).astype(BF16)
        for p in range(GROUP * halves):
            out_ref[pl.ds(at, GROUP), p * WIDE:(p + 1) * WIDE] = got[p * GROUP:p * GROUP + GROUP, :]

    def step(s, carry):
        for u in range(unroll):
            group(s * unroll + u)
        return carry

    lax.fori_loop(0, nodes // (GROUP * unroll), step, 0)


def count_matrix(code, vocab, block=WIDE, unroll=GROUP):
    low, high, _ = code
    n = low.shape[0] * GROUP
    rows = pl.BlockSpec((block // GROUP, WIDE), lambda i: (i, 0))
    return pl.pallas_call(
        functools.partial(count_kernel, vocab // 4096, unroll),
        grid=(n // block,),
        in_specs=[rows, rows],
        out_specs=pl.BlockSpec((block, vocab), lambda i: (i, 0)),
        out_shape=jax.ShapeDtypeStruct((n, vocab), BF16),
        compiler_params=params_of("arbitrary"),
        cost_estimate=pl.CostEstimate(flops=2 * n * vocab * WIDE, bytes_accessed=2 * n * vocab, transcendentals=0),
        name="count_matrix",
    )(low, high)


def norm_rows(z, gain, shift):
    act = jnp.maximum(z, 0.0)
    mean_act = jnp.mean(act, axis=-1, keepdims=True)
    centred = act - mean_act
    var_act = jnp.mean(centred * centred, axis=-1, keepdims=True)
    return centred * lax.rsqrt(var_act + LN_EPS) * gain + shift


def norm_back(z, gain, d_out, axis):
    act = jnp.maximum(z, 0.0)
    mean_act = jnp.mean(act, axis=axis, keepdims=True)
    centred = act - mean_act
    var_act = jnp.mean(centred * centred, axis=axis, keepdims=True)
    inv = lax.rsqrt(var_act + LN_EPS)
    hat = centred * inv
    d_hat = d_out * gain
    mean_d = jnp.mean(d_hat, axis=axis, keepdims=True)
    mean_dh = jnp.mean(d_hat * hat, axis=axis, keepdims=True)
    d_act = (d_hat - mean_d - hat * mean_dh) * inv
    return jnp.where(z > 0.0, d_act, 0.0), d_out * hat


def layer_one_kernel(self_ids, m_ref, codes_ref, *refs):
    part_refs = refs[:SUB]
    (w_self_ref, w_nbr_ref, vec_ref, hs_ref, a_ref, h_ref, zt_ref,
     x_ref, wide_ref, got_ref, hs_old_ref, a_old_ref, z_ref, sems) = refs[SUB:]
    block = m_ref.shape[0]
    rows, feat = x_ref.shape
    pid = pl.program_id(0)
    last = pl.num_programs(0) - 1
    tiles = feat // LANES

    @pl.when(pid == 0)
    def _():
        part = rows // SUB
        copies = [pltpu.make_async_copy(part_refs[p], x_ref.at[pl.ds(p * part, part), :], sems.at[p]) for p in range(SUB)]
        for copy in copies:
            copy.start()

        def spread(s, carry):
            at = pl.multiple_of(s * LANES, LANES)
            for c in range(tiles):
                wide_ref[pl.ds(at * SUB + c, LANES, stride=SUB), :] = x_ref[pl.ds(at, LANES), c * LANES:(c + 1) * LANES].astype(F32)
            return carry
        for p in range(SUB):
            copies[p].wait()
            lax.fori_loop(p * part // LANES, (p + 1) * part // LANES, spread, 0)
        hs_old_ref[...] = jnp.zeros_like(hs_old_ref)
        a_old_ref[...] = jnp.zeros_like(a_old_ref)

    def finish():
        z_ref[...] = (jnp.dot(hs_old_ref[...], w_self_ref[...], preferred_element_type=F32)
                      + jnp.dot(a_old_ref[...], w_nbr_ref[...], preferred_element_type=F32) + vec_ref[0:1, :])
        for at in range(0, block, LANES):
            z = z_ref[at:at + LANES, :]
            h_ref[at:at + LANES, :] = norm_rows(z, vec_ref[1:2, :], vec_ref[2:3, :]).astype(BF16)
            zt_ref[:, at:at + LANES] = z.T

    @pl.when(pid < last)
    def _():
        finish()
        for at in range(block):
            idx = self_ids[pid * block + at]
            got_ref[at * SUB:at * SUB + SUB, :] = wide_ref[pl.ds(pl.multiple_of(idx * SUB, SUB), SUB), :]
        share = 1.0 / codes_ref[:, 0:1]
        for c in range(feat // WIDE):
            cols = slice(c * WIDE, (c + 1) * WIDE)
            acc = jnp.dot(m_ref[...], x_ref[:, cols], preferred_element_type=F32)
            agg = (acc * share).astype(BF16)
            a_ref[:, cols] = agg
            a_old_ref[:, cols] = agg
        for c in range(tiles):
            piece = got_ref[pl.ds(c, block, stride=SUB), :].astype(BF16)
            hs_ref[:, c * LANES:(c + 1) * LANES] = piece
            hs_old_ref[:, c * LANES:(c + 1) * LANES] = piece

    @pl.when(pid == last)
    def _():
        finish()


def layer_one(m_one, code, parts, self_ids, w_self, w_nbr, vecs, block=512):
    n, rows = m_one.shape
    feat = parts[0].shape[1]
    steps = n // block
    whole = lambda i, ids: (0, 0)
    now = lambda i, ids: (jnp.minimum(i, steps - 1), 0)
    old = lambda i, ids: (jnp.maximum(i - 1, 0), 0)
    return pl.pallas_call(
        layer_one_kernel,
        grid_spec=pltpu.PrefetchScalarGridSpec(
            num_scalar_prefetch=1,
            grid=(steps + 1,),
            in_specs=[pl.BlockSpec((block, rows), now),
                      pl.BlockSpec((block, LANES), now)]
            + [pl.BlockSpec(memory_space=pl.ANY)] * SUB
            + [pl.BlockSpec((feat, HIDDEN), whole),
               pl.BlockSpec((feat, HIDDEN), whole),
               pl.BlockSpec((SUB, HIDDEN), whole)],
            out_specs=[pl.BlockSpec((block, feat), now),
                       pl.BlockSpec((block, feat), now),
                       pl.BlockSpec((block, HIDDEN), old),
                       pl.BlockSpec((HIDDEN, block), lambda i, ids: (0, jnp.maximum(i - 1, 0)))],
            scratch_shapes=[pltpu.VMEM((rows, feat), BF16), pltpu.VMEM((rows * SUB, LANES), F32),
                            pltpu.VMEM((block * SUB, LANES), F32), pltpu.VMEM((block, feat), BF16),
                            pltpu.VMEM((block, feat), BF16), pltpu.VMEM((block, HIDDEN), F32),
                            pltpu.SemaphoreType.DMA((SUB,))]),
        out_shape=[jax.ShapeDtypeStruct((n, feat), BF16),
                   jax.ShapeDtypeStruct((n, feat), BF16),
                   jax.ShapeDtypeStruct((n, HIDDEN), BF16),
                   jax.ShapeDtypeStruct((HIDDEN, n), F32)],
        compiler_params=params_of("arbitrary"),
        cost_estimate=pl.CostEstimate(flops=2 * n * rows * feat, bytes_accessed=2 * n * rows, transcendentals=0),
        name="layer_one",
    )(self_ids, m_one, code, *parts, w_self, w_nbr, vecs)


def layer_two_kernel(m_ref, codes_ref, h_all_ref, h_self_ref, w_self_ref, w_nbr_ref, vec_ref, a_ref, h_ref, z_ref):
    share = 1.0 / codes_ref[:, 0:1]
    acc = jnp.dot(m_ref[...], h_all_ref[...], preferred_element_type=F32)
    a_ref[...] = (acc * share).astype(BF16)
    z_ref[...] = (jnp.dot(h_self_ref[...], w_self_ref[...], preferred_element_type=F32)
                  + jnp.dot(a_ref[...], w_nbr_ref[...], preferred_element_type=F32) + vec_ref[0:1, :])
    for at in range(0, m_ref.shape[0], LANES):
        h_ref[at:at + LANES, :] = norm_rows(z_ref[at:at + LANES, :], vec_ref[1:2, :], vec_ref[2:3, :]).astype(BF16)


def layer_two(m_two, code, h_one, w_self, w_nbr, vecs, block=512):
    n, rows = m_two.shape
    whole = lambda i: (0, 0)
    by_row = lambda i: (i, 0)
    return pl.pallas_call(
        layer_two_kernel,
        grid=(n // block,),
        in_specs=[pl.BlockSpec((block, rows), by_row),
                  pl.BlockSpec((block, LANES), by_row),
                  pl.BlockSpec((rows, HIDDEN), whole),
                  pl.BlockSpec((block, HIDDEN), by_row),
                  pl.BlockSpec((HIDDEN, HIDDEN), whole),
                  pl.BlockSpec((HIDDEN, HIDDEN), whole),
                  pl.BlockSpec((SUB, HIDDEN), whole)],
        out_specs=[pl.BlockSpec((block, HIDDEN), by_row)] * 3,
        out_shape=[jax.ShapeDtypeStruct((n, HIDDEN), BF16),
                   jax.ShapeDtypeStruct((n, HIDDEN), BF16),
                   jax.ShapeDtypeStruct((n, HIDDEN), F32)],
        compiler_params=params_of("arbitrary"),
        cost_estimate=pl.CostEstimate(flops=2 * n * rows * HIDDEN, bytes_accessed=2 * n * rows, transcendentals=0),
        name="layer_two",
    )(m_two, code, h_one, h_one, w_self, w_nbr, vecs)


def tdot(lhs, rhs):
    return lax.dot_general(lhs, rhs, (((0,), (0,)), ((), ())), preferred_element_type=F32)


def dot_t(lhs, rhs):
    return lax.dot_general(lhs, rhs, (((1,), (1,)), ((), ())), preferred_element_type=F32)


def put_rows(ref, at, mat):
    n = mat.shape[0]
    ref[pl.ds(at, n, stride=2), :] = mat[:, 0:LANES]
    ref[pl.ds(at + 1, n, stride=2), :] = mat[:, LANES:WIDE]


def put_vector(ref, at, row):
    ref[at:at + 1, :] = row[:, 0:LANES]
    ref[at + 1:at + 2, :] = row[:, LANES:WIDE]


def top_kernel(classes, nbr3_ref, mask3_ref, label_ref, valid_ref, h2_ref, a2_ref, z2_ref, h1_ref, codes2_ref,
               w3s_ref, w3n_ref, w2s_ref, w2n_ref, vec_ref, bias3_ref,
               g3s_ref, g3n_ref, rows_ref, vout_ref, dself_ref, dagg_ref, m3_ref, dh2_ref, dz2_ref):
    fan, seeds = nbr3_ref.shape
    n_two = h2_ref.shape[0]
    piece = 512
    mask3 = mask3_ref[...]
    small = jnp.concatenate([jnp.where(mask3 > 0, nbr3_ref[...], -1), jnp.maximum(jnp.sum(mask3, axis=0, keepdims=True), 1),
                             label_ref[...], valid_ref[...], jnp.zeros((125 - fan, seeds), jnp.int32)], axis=0)
    small = jnp.concatenate([small[:, c * LANES:(c + 1) * LANES].T for c in range(seeds // LANES)], axis=0)
    count3 = small[:, fan:fan + 1].astype(F32)
    for c in range(n_two // piece):
        ids = lax.broadcasted_iota(jnp.int32, (seeds, piece), 1) + c * piece
        acc = jnp.zeros((seeds, piece), F32)
        for k in range(fan):
            acc = acc + jnp.where(ids == small[:, k:k + 1], 1.0, 0.0)
        m3_ref[:, c * piece:(c + 1) * piece] = acc.astype(BF16)
    a3 = (jnp.dot(m3_ref[...], h2_ref[...], preferred_element_type=F32) / count3).astype(BF16)
    self3 = h2_ref[0:seeds, :]
    logits = (jnp.dot(self3, w3s_ref[...], preferred_element_type=F32)
              + jnp.dot(a3, w3n_ref[...], preferred_element_type=F32) + bias3_ref[...])
    col = lax.broadcasted_iota(jnp.int32, logits.shape, 1)
    real = col < classes
    top = jnp.max(jnp.where(real, logits, -jnp.inf), axis=1, keepdims=True)
    powers = jnp.where(real, jnp.exp(logits - top), 0.0)
    total = jnp.sum(powers, axis=1, keepdims=True)
    log_norm = top + jnp.log(total)
    hot = col == small[:, fan + 1:fan + 2]
    picked = jnp.sum(jnp.where(hot, logits, 0.0), axis=1, keepdims=True)
    valid = small[:, fan + 2:fan + 3].astype(F32)
    loss = jnp.sum((log_norm - picked) * valid, axis=0, keepdims=True)
    n_valid = jnp.sum(valid, axis=0, keepdims=True)
    d_logits = (jnp.where(real, jnp.exp(logits - log_norm), 0.0) - jnp.where(hot, 1.0, 0.0)) * valid
    d_logb = d_logits.astype(BF16)
    g3s_ref[...] = tdot(self3, d_logb)
    g3n_ref[...] = tdot(a3, d_logb)
    d_self3 = dot_t(d_logb, w3s_ref[...])
    d_agg3 = (dot_t(d_logb, w3n_ref[...]) / count3).astype(BF16)
    dh2_ref[...] = tdot(m3_ref[...], d_agg3)
    dh2_ref[0:seeds, :] += d_self3
    sums = [jnp.zeros((1, HIDDEN), F32) for _ in range(3)]
    for at in range(0, n_two, LANES):
        span = slice(at, at + LANES)
        d_h2 = dh2_ref[span, :]
        d_z2, gain_terms = norm_back(z2_ref[span, :], vec_ref[1:2, :], d_h2, -1)
        dz2_ref[span, :] = d_z2.astype(BF16)
        for index, term in enumerate((d_z2, gain_terms, d_h2)):
            sums[index] = sums[index] + jnp.sum(term, axis=0, keepdims=True)
    d_bias = jnp.sum(d_logits, axis=0, keepdims=True)
    lane = lax.broadcasted_iota(jnp.int32, (1, LANES), 1)
    rest = classes - LANES
    tail = jnp.where(lane < rest, d_bias[:, LANES:WIDE],
                     jnp.where(lane == rest, loss, jnp.where(lane == rest + 1, n_valid, 0.0)))
    vout_ref[...] = jnp.concatenate([d_bias[:, 0:LANES], tail, jnp.zeros((6, LANES), F32)], axis=0)
    d_z2b = dz2_ref[...]
    put_rows(rows_ref, 0, tdot(h1_ref[...], d_z2b))
    put_rows(rows_ref, 2 * HIDDEN, tdot(a2_ref[...], d_z2b))
    for index in range(3):
        put_vector(rows_ref, 4 * HIDDEN + 2 * index, sums[index])
    rows_ref[4 * HIDDEN + 6:4 * HIDDEN + SUB, :] = jnp.zeros((2, LANES), F32)
    dself_ref[...] = dot_t(d_z2b, w2s_ref[...]).T
    count2 = codes2_ref[:, 0:1]
    dagg_ref[...] = (dot_t(d_z2b, w2n_ref[...]) / count2).T.astype(BF16)


def top(classes, nbr3, mask3, label, valid, h2, a2, z2, h1, codes2, w3s, w3n, w2s, w2n, vecs, bias3):
    n_two = h2.shape[0]
    seeds = nbr3.shape[1]
    square = jax.ShapeDtypeStruct((HIDDEN, HIDDEN), F32)
    rows = jax.ShapeDtypeStruct((4 * HIDDEN + SUB, LANES), F32)
    full = lambda x: pl.BlockSpec(x.shape, lambda i: (0, 0))
    args = (nbr3, mask3, label, valid, h2, a2, z2, h1, codes2, w3s, w3n, w2s, w2n, vecs, bias3)
    outs = [square, square, rows, jax.ShapeDtypeStruct((SUB, LANES), F32),
            jax.ShapeDtypeStruct((HIDDEN, n_two), F32), jax.ShapeDtypeStruct((HIDDEN, n_two), BF16)]
    specs = [full(x) for x in args]
    specs[7] = pl.BlockSpec((n_two, HIDDEN), lambda i: (0, 0))
    return pl.pallas_call(
        functools.partial(top_kernel, classes),
        grid=(1,),
        in_specs=specs,
        out_specs=[full(x) for x in outs],
        out_shape=outs,
        scratch_shapes=[pltpu.VMEM((seeds, n_two), BF16), pltpu.VMEM((n_two, HIDDEN), F32),
                        pltpu.VMEM((n_two, HIDDEN), BF16)],
        compiler_params=params_of("arbitrary"),
        name="layer_three",
    )(*args)


def bottom_kernel(dagg_ref, m_ref, dself_ref, zt_ref, hs_ref, a_ref, gain_ref, rows_ref,
                  gs_ref, gn_ref, vec_ref, dz_ref, dh_ref):
    pid = pl.program_id(0)
    last = pl.num_programs(0) - 1
    block = m_ref.shape[1]
    feat = hs_ref.shape[1]
    n_self = dself_ref.shape[1] // block

    @pl.when(pid == 0)
    def _():
        gs_ref[...] = jnp.zeros_like(gs_ref)
        gn_ref[...] = jnp.zeros_like(gn_ref)
        vec_ref[...] = jnp.zeros_like(vec_ref)
        dz_ref[...] = jnp.zeros_like(dz_ref)

    def weights():
        gs_ref[...] += jnp.dot(dz_ref[...], hs_ref[...], preferred_element_type=F32)
        gn_ref[...] += jnp.dot(dz_ref[...], a_ref[...], preferred_element_type=F32)

    @pl.when(pid < last)
    def _():
        weights()
        dh_ref[...] = jnp.dot(dagg_ref[...], m_ref[...], preferred_element_type=F32)

        @pl.when(pid < n_self)
        def _():
            dh_ref[...] += dself_ref[:, pl.ds(pl.multiple_of(pid * block, block), block)]

        for at in range(0, block, LANES):
            span = slice(at, at + LANES)
            d_h = dh_ref[:, span]
            d_z, gain_terms = norm_back(zt_ref[:, span], gain_ref[:, 0:1], d_h, 0)
            dz_ref[:, span] = d_z.astype(BF16)
            for index, term in enumerate((d_z, gain_terms, d_h)):
                vec_ref[index] += term

    @pl.when(pid == last)
    def _():
        weights()
        put_rows(rows_ref, 0, gs_ref[...].T)
        put_rows(rows_ref, 2 * feat, gn_ref[...].T)
        for index in range(3):
            put_vector(rows_ref, 4 * feat + 2 * index, jnp.sum(vec_ref[index].T, axis=0, keepdims=True))
        rows_ref[4 * feat + 6:4 * feat + SUB, :] = jnp.zeros((2, LANES), F32)


def bottom(dagg_t, m_two, dself_t, z_t, h_self, a_one, gain_col, block=1024):
    n_two, n = m_two.shape
    feat = h_self.shape[1]
    whole = lambda i: (0, 0)
    rows = 4 * feat + SUB
    steps = n // block
    now = lambda i: (0, jnp.minimum(i, steps - 1))
    old = lambda i: (jnp.maximum(i - 1, 0), 0)
    return pl.pallas_call(
        bottom_kernel,
        grid=(steps + 1,),
        in_specs=[pl.BlockSpec((HIDDEN, n_two), whole),
                  pl.BlockSpec((n_two, block), now),
                  pl.BlockSpec((HIDDEN, n_two), whole),
                  pl.BlockSpec((HIDDEN, block), now),
                  pl.BlockSpec((block, feat), old),
                  pl.BlockSpec((block, feat), old),
                  pl.BlockSpec((HIDDEN, LANES), whole)],
        out_specs=pl.BlockSpec((rows, LANES), whole),
        out_shape=jax.ShapeDtypeStruct((rows, LANES), F32),
        scratch_shapes=[pltpu.VMEM((HIDDEN, feat), F32), pltpu.VMEM((HIDDEN, feat), F32), pltpu.VMEM((3, HIDDEN, LANES), F32),
                        pltpu.VMEM((HIDDEN, block), BF16), pltpu.VMEM((HIDDEN, block), F32)],
        compiler_params=params_of("arbitrary"),
        cost_estimate=pl.CostEstimate(flops=2 * n * n_two * HIDDEN, bytes_accessed=2 * n * n_two, transcendentals=0),
        name="layer_one_back",
    )(dagg_t, m_two, dself_t, z_t, h_self, a_one, gain_col)


CHUNKS = 2
PHASES = 5


def sum_kernel(low_ref, mid_ref, top_ref, next_ref, tail_ref, out_ref, buf_ref, in0_ref, in1_ref, in2_ref, send_sem, recv_sem):
    me = lax.axis_index('dp')
    core = me % 2
    x_bit = (me // 2) % 2
    y_bit = me // 4
    x_peer = me + 2 - 4 * x_bit
    y_peer = me + 4 - SUB * y_bit
    mate = me + 1 - 2 * core
    first = x_bit + core * (y_bit - x_bit)
    peer_one = x_peer + core * (y_peer - x_peer)
    peer_two = y_peer + core * (x_peer - y_peer)
    barrier = pltpu.get_barrier_semaphore()
    for peer in (mate, x_peer, y_peer):
        pl.semaphore_signal(barrier, inc=1, device_id=(peer,), device_id_type=pl.DeviceIdType.MESH)
    at = 0
    for ref, count in ((low_ref, low_ref.shape[0] - 2), (mid_ref, mid_ref.shape[0] - 2),
                       (top_ref, top_ref.shape[0]), (next_ref, next_ref.shape[0]), (tail_ref, SUB)):
        buf_ref[at:at + count, :] = ref[0:count, :]
        at += count
    if at < buf_ref.shape[0]:
        buf_ref[at:, :] = jnp.zeros((buf_ref.shape[0] - at, LANES), F32)
    pl.semaphore_wait(barrier, 3)

    size = buf_ref.shape[0] // CHUNKS
    half, quarter = size // 2, size // 4

    def rows(ref, at, count):
        return ref.at[pl.ds(pl.multiple_of(at, SUB), count), :]

    def copy(chunk, phase):
        base = chunk * size + core * half
        if phase == 0:
            src, dst, peer = rows(buf_ref, chunk * size + (1 - core) * half, half), in0_ref.at[chunk], mate
        elif phase == 1:
            src, dst, peer = rows(buf_ref, base + (1 - first) * quarter, quarter), in1_ref.at[chunk], peer_one
        elif phase == 2:
            src, dst, peer = rows(buf_ref, base + first * quarter, quarter), in2_ref.at[chunk], peer_two
        elif phase == 3:
            at = base + first * quarter
            src, dst, peer = rows(out_ref, at, quarter), rows(out_ref, at, quarter), peer_one
        else:
            src, dst, peer = rows(out_ref, base, half), rows(out_ref, base, half), mate
        return pltpu.make_async_remote_copy(
            src_ref=src, dst_ref=dst, send_sem=send_sem.at[chunk, phase], recv_sem=recv_sem.at[chunk, phase],
            device_id=(peer,), device_id_type=pl.DeviceIdType.MESH)

    def absorb(chunk, phase):
        base = chunk * size + core * half
        if phase == 0:
            at = pl.ds(pl.multiple_of(base, SUB), half)
            buf_ref[at, :] = buf_ref[at, :] + in0_ref[chunk]
        elif phase == 1:
            at = pl.ds(pl.multiple_of(base + first * quarter, SUB), quarter)
            buf_ref[at, :] = buf_ref[at, :] + in1_ref[chunk]
        elif phase == 2:
            at = pl.ds(pl.multiple_of(base + first * quarter, SUB), quarter)
            out_ref[at, :] = buf_ref[at, :] + in2_ref[chunk]

    copies = {}
    for tick in range(PHASES + CHUNKS):
        for chunk in range(CHUNKS):
            phase = tick - chunk
            if 0 < phase <= PHASES:
                copies[chunk, phase - 1].wait_recv()
                absorb(chunk, phase - 1)
            if 0 <= phase < PHASES:
                copies[chunk, phase] = copy(chunk, phase)
                copies[chunk, phase].start()
    for done in copies.values():
        done.wait_send()


def sum_devices(*pieces):
    used = sum(piece.shape[0] for piece in pieces) - 4
    unit = 32 * CHUNKS
    n = -(-used // unit) * unit
    vmem = pl.BlockSpec(memory_space=pltpu.VMEM)
    size = n // CHUNKS
    return pl.pallas_call(
        sum_kernel,
        in_specs=[vmem] * 5,
        out_specs=vmem,
        out_shape=jax.ShapeDtypeStruct((n, LANES), F32),
        scratch_shapes=[pltpu.VMEM((n, LANES), F32),
                        pltpu.VMEM((CHUNKS, size // 2, LANES), F32),
                        pltpu.VMEM((CHUNKS, size // 4, LANES), F32),
                        pltpu.VMEM((CHUNKS, size // 4, LANES), F32),
                        pltpu.SemaphoreType.DMA((CHUNKS, PHASES)),
                        pltpu.SemaphoreType.DMA((CHUNKS, PHASES))],
        compiler_params=pltpu.CompilerParams(collective_id=1, has_side_effects=True, vmem_limit_bytes=VMEM_ALL),
        name="sum_devices",
    )(*pieces)


def adam_update(params, adam_m, adam_v, grads):
    m_new = BETA_ONE * adam_m + (1.0 - BETA_ONE) * grads
    v_new = BETA_TWO * adam_v + (1.0 - BETA_TWO) * grads * grads
    m_hat = m_new / (1.0 - BETA_ONE ** STEP)
    v_hat = v_new / (1.0 - BETA_TWO ** STEP)
    return (params - ADAM_LR * m_hat / (jnp.sqrt(v_hat) + ADAM_EPS), m_new, v_new)


def swap(x, bit):
    return lax.ppermute(x, 'dp', [(i, i ^ bit) for i in range(SUB)])


def weights_kernel(rows_ref, s1_ref, n1_ref, s2_ref, n2_ref, vec_ref, gain_ref):
    at = 0
    for ref in (s1_ref, n1_ref, None, s2_ref, n2_ref):
        if ref is None:
            at += 6
            continue
        n = ref.shape[0]
        ref[:, 0:LANES] = rows_ref[pl.ds(at, n, stride=2), :].astype(BF16)
        ref[:, LANES:WIDE] = rows_ref[pl.ds(at + 1, n, stride=2), :].astype(BF16)
        at += 2 * n
    feat = s1_ref.shape[0]
    for layer, base in enumerate((4 * feat, at)):
        for index in range(3):
            row = jnp.concatenate([rows_ref[base + 2 * index:base + 2 * index + 1, :],
                                   rows_ref[base + 2 * index + 1:base + 2 * index + 2, :]], axis=1)
            vec_ref[layer * SUB + index:layer * SUB + index + 1, :] = row
        vec_ref[layer * SUB + 3:layer * SUB + SUB, :] = jnp.zeros((5, HIDDEN), F32)
    gain_ref[...] = jnp.broadcast_to(vec_ref[1:2, :], (LANES, HIDDEN)).T


def weights(rows, feat):
    wide = jax.ShapeDtypeStruct((feat, HIDDEN), BF16)
    square = jax.ShapeDtypeStruct((HIDDEN, HIDDEN), BF16)
    vmem = pl.BlockSpec(memory_space=pltpu.VMEM)
    return pl.pallas_call(
        weights_kernel,
        in_specs=[vmem],
        out_specs=[vmem] * 6,
        out_shape=[wide, wide, square, square, jax.ShapeDtypeStruct((GROUP, HIDDEN), F32),
                   jax.ShapeDtypeStruct((HIDDEN, LANES), F32)],
        compiler_params=pltpu.CompilerParams(vmem_limit_bytes=VMEM_ALL),
        name="weights",
    )(rows)


def solution(mesh):
    def body(feats, frontier, nbr_l1, mask_l1, nbr_l2, mask_l2, nbr_l3, mask_l3, labels, seed_mask, params, adam_m, adam_v):
        feat = feats.shape[1]
        classes = class_count(params.shape[0], feat)
        n_one = nbr_l1.shape[0]
        rows_dev = feats.shape[0]
        groups = mesh.shape['dp']
        by_x = swap(feats, 2)
        by_y = swap(feats, 4)
        front = frontier ^ (lax.axis_index('dp') * rows_dev)
        used = (4 * feat + 4 * HIDDEN + 12) * LANES
        ws1, wn1, ws2, wn2, vecs, gain_col = weights(params[:used].reshape(-1, LANES), feat)
        span = HIDDEN * classes
        pad3 = ((0, 0), (0, HIDDEN - classes))
        w3s = jnp.pad(params[used:used + span].reshape(HIDDEN, classes).astype(BF16), pad3)
        w3n = jnp.pad(params[used + span:used + 2 * span].reshape(HIDDEN, classes).astype(BF16), pad3)
        bias3 = jnp.pad(params[used + 2 * span:].reshape(1, classes), ((0, 0), (0, HIDDEN - classes)))
        code_one = compose(front, nbr_l1.T, mask_l1.T)
        code_two = codes(nbr_l2.T, mask_l2.T, 256.0)
        code_one, by_x, by_y = lax.optimization_barrier((code_one, by_x, by_y))
        by_xy = swap(by_x, 4)
        m_one = count_matrix(code_one, groups * rows_dev)
        code_two, by_xy, m_one = lax.optimization_barrier((code_two, by_xy, m_one))
        parts = []
        for part in (feats, by_x, by_y, by_xy):
            parts += [part, swap(part, 1)]
        m_two = count_matrix(code_two, n_one)
        h_self, a_one, h_one, z_one_t = layer_one(m_one, code_one[2], parts, front[:n_one], ws1, wn1, vecs[:SUB])
        a_two, h_two, z_two = layer_two(m_two, code_two[2], h_one, ws2, wn2, vecs[SUB:])
        g3s, g3n, mid_rows, vout, dself_t, dagg_t = top(
            classes, nbr_l3.T, mask_l3.T, labels[None, :], seed_mask[None, :], h_two, a_two, z_two, h_one, code_two[2],
            w3s, w3n, ws2, wn2, vecs[SUB:], bias3)
        low_rows = bottom(dagg_t, m_two, dself_t, z_one_t, h_self, a_one, gain_col)
        n_params = params.shape[0]
        flat3 = [g[:, :classes].reshape(-1).reshape(-1, LANES) for g in (g3s, g3n)]
        sums = sum_devices(low_rows, mid_rows, *flat3, vout).reshape(-1)
        total = jnp.maximum(sums[n_params + 1], 1.0)
        loss = sums[n_params] / total
        return (loss,) + adam_update(params, adam_m, adam_v, sums[:n_params] / total)

    row_spec = P('dp')
    replicated = P()
    return jax.shard_map(body, mesh=mesh, in_specs=(row_spec,) * 10 + (replicated,) * 3,
                         out_specs=(replicated,) * 4, check_vma=False)
```

time: 349 us -> 300 us (0.86)
  Pallas kernels: 293 us -> 265 us
  local copies, waits for them, and re-layouts: 28.8 us -> 14.3 us
  between operations: 16.6 us -> 3.2 us
  starting transfers between devices: 0.04 us -> 6.17 us
    pallas_call x1, Pallas kernels: 98.2 us -> 81.3 us  [layer_one(): pl.pallas_call(layer_one_kernel, grid_spec=pltpu.PrefetchScalarGridSpec(n...]
    concatenate x1 -> x0, local copies, waits for them, and re-layouts: 7.13 us -> none  [body(): jnp.concatenate([g3s[:, :classes].reshape(-1), g3n[:, :classes].reshape(-...]
    ppermute x0 -> x7, starting transfers between devices: none -> 6.17 us  [swap(): return lax.ppermute(x, 'dp', [(i, i ^ bit) for i in range(SUB)])]
    pallas_call x2 -> x3, Pallas kernels: 77.8 us -> 72.7 us  [the longest x1 36 us: sum_devices(): pl.pallas_call(sum_kernel, in_specs=[vmem] * 5, out_specs=vmem, out_shape...]
    pallas_call x2, Pallas kernels: 50.3 us -> 45.3 us  [count_matrix(): pl.pallas_call(functools.partial(count_kernel, vocab // 4096, unroll), gr...]
  transfers between devices with their start and end apart: 1 -> 7, of which waited for: 0 -> 0; matrix products, arithmetic and copies ran while one was open for 5% -> 3% of each run, Pallas kernels for 24% -> 27%
where the time goes in v3:
time: 300 us; the launch traced here: 298 us
  Pallas kernels  265 us (88%)
  local copies, waits for them, and re-layouts  14.3 us (5%)
  other arithmetic  8.91 us (3%)
  starting transfers between devices  6.17 us (2%)
  between operations  3.2 us (1%)
    pallas_call x1, Pallas kernels, layer_one(): pl.pallas_call(layer_one_kernel, grid_spec=pltpu.PrefetchScalarGridSpec(n...  81.3 us
    pallas_call x2, Pallas kernels, count_matrix(): pl.pallas_call(functools.partial(count_kernel, vocab // 4096, unroll), gr...  45.3 us
    pallas_call x1, Pallas kernels, sum_devices(): pl.pallas_call(sum_kernel, in_specs=[vmem] * 5, out_specs=vmem, out_shape...  36 us
    pallas_call x1, Pallas kernels, bottom(): pl.pallas_call(bottom_kernel, grid=(steps + 1,), in_specs=[pl.BlockSpec((...  33.9 us
    pallas_call x1, Pallas kernels, compose(): pl.pallas_call(compose_kernel, grid=(n // block,), in_specs=[pl.BlockSpec...  29.5 us
    pallas_call x1, Pallas kernels, layer_two(): pl.pallas_call(layer_two_kernel, grid=(n // block,), in_specs=[pl.BlockSp...  20.8 us
    pallas_call x1, Pallas kernels, top(): pl.pallas_call(functools.partial(top_kernel, classes), grid=(1,), in_spec...  12.3 us
    sub x1, other arithmetic, adam_update(): params - ADAM_LR * m_hat / (jnp.sqrt(v_hat) + ADAM_EPS)  7.09 us
  transfers between devices with their start and end apart: 7, of which 0 were waited for; matrix products, arithmetic and copies ran while one was open for 3% of the time, Pallas kernels for 27%

profile of v3, /device:TPU:0, one launch (start us, length us, event | category | flops | bytes accessed | tf_op | source)
XLA Modules:
  0.0 298.1 jit_solution(11945978484985340525)
XLA Ops:
  0.6 0.0 copy-start
  0.6 3.4 %collective-permute-start = (bf16[512,768]{1,0:T(8,128)(2,1)}, bf16[512,768]{1,0:T(8,128)(2,1)S(1)}, u32[]{:S(2)}, u32[]{:S(2)}) collective-permute-start(bf16[512,768]{1,0:T(8,128)(2,1)} %refs_0_.1), channel_id=1, source_target_pairs={{0,2},{1,3},{2,0},{3,1},{4,6},{5,7},{6,4},{7,5}} | collective-permute-start | bytes 2359304 | tf_op jit(solution)/shard_map/ppermute | solution.py:621
  4.0 1.5 collective-permute-start.1
  5.5 0.0 collective-permute-start.3
  5.5 3.0 %slice_bitcast_fusion.rows_ref = f32[4108,128]{1,0:T(8,128)} fusion(f32[604313]{0:T(1024)} %param.23), kind=kLoop, calls=%fused_computation.5 | loop fusion | bytes 4206592 | tf_op jit(solution)/shard_map/reshape | solution.py:670
  8.6 0.0 copy-done
  8.6 0.0 copy-start.2
  8.6 1.1 convert.4
  9.7 2.7 weights.1
  12.5 1.0 fusion.3
  13.5 0.0 copy-done.2
  13.5 0.7 fusion.5.front_ref
  14.1 0.0 slice-start
  14.1 0.0 copy-start.3
  14.1 29.5 %compose_ids.1 = (f32[512,256]{1,0:T(8,128)}, f32[512,256]{1,0:T(8,128)}, f32[8192,128]{1,0:T(8,128)}) custom-call(s32[256,128]{1,0:T(8,128)} %fusion.5.front_ref, s32[15,8192]{1,0:T(8,128)} %bitcast.29, s32[15,8192]{1,0:T(8,128)} %bitcast.30), custom_call_target="tpu_custom_call" | custom-call | flops 16106127360 | bytes 10000000 | tf_op jit(solution)/shard_map/compose_ids/pallas_call | solution.py:110
  43.6 0.6 slice.51.self_ids
  44.2 0.4 convert_element_type.13
  44.6 0.4 convert_element_type.14
  45.0 0.7 pad.11.w3s_ref
  45.7 0.7 pad.12.w3n_ref
  46.3 3.6 %codes.1 = (f32[128,256]{1,0:T(8,128)}, f32[128,256]{1,0:T(8,128)}, f32[2048,128]{1,0:T(8,128)}) custom-call(s32[10,2048]{1,0:T(8,128)} %bitcast.23, s32[10,2048]{1,0:T(8,128)} %bitcast.24), custom_call_target="tpu_custom_call" | custom-call | tf_op jit(solution)/shard_map/codes/pallas_call | solution.py:126
  49.9 0.0 slice-done
  49.9 0.6 pad.13.bias3_ref
  50.5 0.0 copy-done.3
  50.5 0.6 fusion.4
  51.1 0.0 collective-permute-done.refs_2_
  51.1 0.0 copy-start.4
  51.1 0.0 collective-permute-done.1.refs_4_
  51.1 0.5 collective-permute-start.2
  51.7 0.2 collective-permute-start.4
  51.9 0.3 collective-permute-start.5
  52.2 32.1 %count_matrix.2.m_ref = bf16[8192,4096]{1,0:T(8,128)(2,1)} custom-call(f32[512,256]{1,0:T(8,128)} %get-tuple-element.46.low_ref, f32[512,256]{1,0:T(8,128)} %get-tuple-element.47.high_ref), custom_call_target="tpu_custom_call" | custom-call | flops 17179869184 | bytes 67108864 | tf_op jit(solution)/shard_map/count_matrix/pallas_call | solution.py:169
  84.3 0.0 copy-done.4
  84.3 0.0 collective-permute-done.2.refs_6_
  84.3 0.0 copy-start.5
  84.3 0.2 collective-permute-start.6
  84.6 13.2 %count_matrix.3.m_ref = bf16[2048,8192]{1,0:T(8,128)(2,1)} custom-call(f32[128,256]{1,0:T(8,128)} %get-tuple-element.48.low_ref, f32[128,256]{1,0:T(8,128)} %get-tuple-element.49.high_ref), custom_call_target="tpu_custom_call" | custom-call | flops 8589934592 | bytes 33554432 | tf_op jit(solution)/shard_map/count_matrix/pallas_call | solution.py:169
  97.8 0.0 copy-done.5
  97.8 0.0 collective-permute-done.3.refs_1_
  97.8 0.0 collective-permute-done.4.refs_3_
  97.8 0.0 copy-start.6
  97.8 0.0 collective-permute-done.5.refs_5_
  97.8 0.0 copy-start.7
  97.8 0.0 collective-permute-done.6.refs_7_
  97.8 0.8 copy-done.6
  98.7 0.3 copy-done.7
  99.0 81.3 %layer_one.1 = (bf16[8192,768]{1,0:T(8,128)(2,1)}, bf16[8192,768]{1,0:T(8,128)(2,1)}, bf16[8192,256]{1,0:T(8,128)(2,1)}, f32[256,8192]{1,0:T(8,128)}) custom-call(s32[8192]{0:T(1024)} %slice.51.self_ids, bf16[8192,4096]{1,0:T(8,128)(2,1)} %count_matrix.2.m_ref, f32[8192,128]{1,0:T(8,128)} %get-tuple-element.52.codes_ref, bf16[512,768]{1,0:T(8,128)(2,1)} %refs_0_.1, ...), custom_call_target="tpu_custom_call" | custom-call | flops 51539607552 | bytes 67108864 | tf_op jit(solution)/shard_map/layer_one/pallas_call | solution.py:269
  180.3 20.8 %layer_two.1 = (bf16[2048,256]{1,0:T(8,128)(2,1)}, bf16[2048,256]{1,0:T(8,128)(2,1)}, f32[2048,256]{1,0:T(8,128)}) custom-call(bf16[2048,8192]{1,0:T(8,128)(2,1)} %count_matrix.3.m_ref, f32[2048,128]{1,0:T(8,128)} %get-tuple-element.50.codes_ref.codes2_ref, bf16[8192,256]{1,0:T(8,128)(2,1)} %get-tuple-element.58.h_all_ref.h_self_ref.h1_ref, ...), custom_call_target="tpu_custom_call" | custom-call | flops 8589934592 | bytes 33554432 | tf_op jit(solution)/shard_map/layer_two/pallas_call | solution.py:312
  201.1 12.3 %layer_three.1 = (f32[256,256]{1,0:T(8,128)}, f32[256,256]{1,0:T(8,128)}, f32[1032,128]{1,0:T(8,128)}, f32[8,128]{1,0:T(8,128)}, f32[256,2048]{1,0:T(8,128)}, /*index=5*/bf16[256,2048]{1,0:T(8,128)(2,1)}) custom-call(s32[5,512]{1,0:T(8,128)} %bitcast.25, s32[5,512]{1,0:T(8,128)} %bitcast.26, s32[1,512]{1,0:T(1,128)} %bitcast.27, s32[1,512]{1,0:T(1,128)} %bitcast.28, ...), custom_call_target="tpu_custom_call" | custom-call | tf_op jit(solution)/shard_map/layer_three/pallas_call | solution.py:427
  213.4 1.9 reshape_reshape.6.top_ref
  215.3 1.9 reshape_reshape.7.next_ref
  217.3 33.9 %layer_one_back.1.low_ref = f32[3080,128]{1,0:T(8,128)} custom-call(bf16[256,2048]{1,0:T(8,128)(2,1)} %get-tuple-element.64.dagg_ref, bf16[2048,8192]{1,0:T(8,128)(2,1)} %count_matrix.3.m_ref, f32[256,2048]{1,0:T(8,128)} %get-tuple-element.65.dself_ref, f32[256,8192]{1,0:T(8,128)} %get-tuple-element.66.zt_ref, bf16[8192,768]{1,0:T(8,128)(2,1)} %get-tuple-element.67.hs_ref, ...), custom_call_target="tpu_custom_call" | custom-call | flops 8589934592 | bytes 33554432 | tf_op jit(solution)/shard_map/layer_one_back/pallas_call | solution.py:494
  251.2 0.0 copy-start.1
  251.2 36.0 %sum_devices.1 = f32[4736,128]{1,0:T(8,128)} custom-call(f32[3080,128]{1,0:T(8,128)} %layer_one_back.1.low_ref, f32[1032,128]{1,0:T(8,128)} %get-tuple-element.70.mid_ref, f32[306,128]{1,0:T(8,128)} %reshape_reshape.6.top_ref, f32[306,128]{1,0:T(8,128)} %reshape_reshape.7.next_ref, f32[8,128]{1,0:T(8,128)} %get-tuple-element.73.tail_ref), custom_call_target="tpu_custom_call" | custom-call | tf_op jit(solution)/shard_map/sum_devices/pallas_call | solution.py:596
  287.2 1.3 fusion.2
  289.8 0.0 copy-done.1
  289.9 7.1 %divide_subtract_fusion = (f32[604313]{0:T(1024)}, f32[604313]{0:T(1024)}, f32[604313]{0:T(1024)}) fusion(f32[604313]{0:T(1024)S(1)} %copy-done.1, f32[]{:T(128)} %bitcast.13, f32[606208]{0:T(1024)} %bitcast.20, f32[604313]{0:T(1024)} %param.24, f32[604313]{0:T(1024)} %param.25), kind=kLoop, calls=%fused_computation.3 | loop fusion | flops 7856069 | bytes 16920768 | tf_op jit(solution)/shard_map/sub | solution.py:617
  (1 shorter events, 0.0 us)
Async XLA Ops:
  0.6 8.0 %copy-start = (f32[604313]{0:T(1024)S(1)}, f32[604313]{0:T(1024)}, u32[]{:S(2)}) copy-start(f32[604313]{0:T(1024)} %param.23) | copy-start | bytes 7251760
  0.6 50.5 %collective-permute-start = (bf16[512,768]{1,0:T(8,128)(2,1)}, bf16[512,768]{1,0:T(8,128)(2,1)S(1)}, u32[]{:S(2)}, u32[]{:S(2)}) collective-permute-start(bf16[512,768]{1,0:T(8,128)(2,1)} %refs_0_.1), channel_id=1, source_target_pairs={{0,2},{1,3},{2,0},{3,1},{4,6},{5,7},{6,4},{7,5}} | collective-permute-start | bytes 2359304 | tf_op jit(solution)/shard_map/ppermute | solution.py:621
  4.0 47.1 %collective-permute-start.1 = (bf16[512,768]{1,0:T(8,128)(2,1)}, bf16[512,768]{1,0:T(8,128)(2,1)}, u32[]{:S(2)}, u32[]{:S(2)}) collective-permute-start(bf16[512,768]{1,0:T(8,128)(2,1)} %refs_0_.1), channel_id=1, source_target_pairs={{0,4},{1,5},{2,6},{3,7},{4,0},{5,1},{6,2},{7,3}} | collective-permute-start | bytes 2359304 | tf_op jit(solution)/shard_map/ppermute | solution.py:621
  5.5 92.3 %collective-permute-start.3 = (bf16[512,768]{1,0:T(8,128)(2,1)}, bf16[512,768]{1,0:T(8,128)(2,1)}, u32[]{:S(2)}, u32[]{:S(2)}) collective-permute-start(bf16[512,768]{1,0:T(8,128)(2,1)} %refs_0_.1), channel_id=1, source_target_pairs={{0,1},{1,0},{2,3},{3,2},{4,5},{5,4},{6,7},{7,6}} | collective-permute-start | bytes 2359304 | tf_op jit(solution)/shard_map/ppermute | solution.py:621
  8.6 4.9 %copy-start.2 = (s32[32768]{0:T(1024)S(1)}, s32[32768]{0:T(1024)}, u32[]{:S(2)}) copy-start(s32[32768]{0:T(1024)} %param.14) | copy-start | bytes 393220
  14.1 35.8 %slice-start = ((f32[604313]{0:T(1024)}), f32[153]{0:T(256)S(1)}, s32[]{:S(2)}) async-start(f32[604313]{0:T(1024)} %param.23), calls=%async_computation | async-start | bytes 2048 | tf_op jit(solution)/shard_map/slice | solution.py:675
  14.1 36.4 %copy-start.3 = (f32[16,256]{1,0:T(8,128)S(1)}, f32[16,256]{1,0:T(8,128)}, u32[]{:S(2)}) copy-start(f32[16,256]{1,0:T(8,128)} %get-tuple-element.57) | copy-start | bytes 49156
  51.1 33.2 %copy-start.4 = (bf16[512,768]{1,0:T(8,128)(2,1)}, bf16[512,768]{1,0:T(8,128)(2,1)S(1)}, u32[]{:S(2)}) copy-start(bf16[512,768]{1,0:T(8,128)(2,1)S(1)} %collective-permute-done.refs_2_) | copy-start | bytes 2359300
  51.1 33.2 %collective-permute-start.2 = (bf16[512,768]{1,0:T(8,128)(2,1)S(1)}, bf16[512,768]{1,0:T(8,128)(2,1)S(1)}, u32[]{:S(2)}, u32[]{:S(2)}) collective-permute-start(bf16[512,768]{1,0:T(8,128)(2,1)S(1)} %collective-permute-done.refs_2_), channel_id=1, source_target_pairs={{0,4},{1,5},{2,6},{3,7},{4,0},{5,1},{6,2},{7,3}} | collective-permute-start | bytes 2359304 | tf_op jit(solution)/shard_map/ppermute | solution.py:621
  51.7 46.1 %collective-permute-start.4 = (bf16[512,768]{1,0:T(8,128)(2,1)S(1)}, bf16[512,768]{1,0:T(8,128)(2,1)S(1)}, u32[]{:S(2)}, u32[]{:S(2)}) collective-permute-start(bf16[512,768]{1,0:T(8,128)(2,1)S(1)} %collective-permute-done.refs_2_), channel_id=1, source_target_pairs={{0,1},{1,0},{2,3},{3,2},{4,5},{5,4},{6,7},{7,6}} | collective-permute-start | bytes 2359304 | tf_op jit(solution)/shard_map/ppermute | solution.py:621
  51.9 45.9 %collective-permute-start.5 = (bf16[512,768]{1,0:T(8,128)(2,1)}, bf16[512,768]{1,0:T(8,128)(2,1)S(1)}, u32[]{:S(2)}, u32[]{:S(2)}) collective-permute-start(bf16[512,768]{1,0:T(8,128)(2,1)} %collective-permute-done.1.refs_4_), channel_id=1, source_target_pairs={{0,1},{1,0},{2,3},{3,2},{4,5},{5,4},{6,7},{7,6}} | collective-permute-start | bytes 2359304 | tf_op jit(solution)/shard_map/ppermute | solution.py:621
  84.3 13.5 %copy-start.5 = (bf16[512,768]{1,0:T(8,128)(2,1)}, bf16[512,768]{1,0:T(8,128)(2,1)S(1)}, u32[]{:S(2)}) copy-start(bf16[512,768]{1,0:T(8,128)(2,1)S(1)} %collective-permute-done.2.refs_6_) | copy-start | bytes 2359300
  84.3 13.5 %collective-permute-start.6 = (bf16[512,768]{1,0:T(8,128)(2,1)S(1)}, bf16[512,768]{1,0:T(8,128)(2,1)}, u32[]{:S(2)}, u32[]{:S(2)}) collective-permute-start(bf16[512,768]{1,0:T(8,128)(2,1)S(1)} %collective-permute-done.2.refs_6_), channel_id=1, source_target_pairs={{0,1},{1,0},{2,3},{3,2},{4,5},{5,4},{6,7},{7,6}} | collective-permute-start | bytes 2359304 | tf_op jit(solution)/shard_map/ppermute | solution.py:621
  97.8 0.9 copy-start.6
  97.8 1.1 copy-start.7
  251.2 38.7 %copy-start.1 = (f32[604313]{0:T(1024)S(1)}, f32[604313]{0:T(1024)}, u32[]{:S(2)}) copy-start(f32[604313]{0:T(1024)} %param.23) | copy-start | bytes 7251760

commit v4 on v3

--- a/solution.py
+++ b/solution.py
@@ -104,7 +104,7 @@
                 out_shape=[shape, shape, jax.ShapeDtypeStruct((n, LANES), F32)])
 
 
-def compose(frontier, nbr_t, mask_t, block=512):
+def compose(frontier, nbr_t, mask_t, block=2048):
     fan, n = nbr_t.shape
     rows = frontier.shape[0] // LANES
     return pl.pallas_call(
@@ -121,7 +121,7 @@
     )(frontier.reshape(rows, LANES), nbr_t, mask_t)
 
 
-def codes(nbr_t, mask_t, shift, block=512):
+def codes(nbr_t, mask_t, shift, block=1024):
     fan, n = nbr_t.shape
     return pl.pallas_call(
         functools.partial(codes_kernel, shift),
@@ -162,7 +162,7 @@
     lax.fori_loop(0, nodes // (GROUP * unroll), step, 0)
 
 
-def count_matrix(code, vocab, block=WIDE, unroll=GROUP):
+def count_matrix(code, vocab, block=512, unroll=32):
     low, high, _ = code
     n = low.shape[0] * GROUP
     rows = pl.BlockSpec((block // GROUP, WIDE), lambda i: (i, 0))
@@ -677,7 +677,7 @@
         code_two = codes(nbr_l2.T, mask_l2.T, 256.0)
         code_one, by_x, by_y = lax.optimization_barrier((code_one, by_x, by_y))
         by_xy = swap(by_x, 4)
-        m_one = count_matrix(code_one, groups * rows_dev)
+        m_one = count_matrix(code_one, groups * rows_dev, 1024, 64)
         code_two, by_xy, m_one = lax.optimization_barrier((code_two, by_xy, m_one))
         parts = []
         for part in (feats, by_x, by_y, by_xy):

time: 300 us -> 286 us (0.953)
  Pallas kernels: 265 us -> 253 us
    pallas_call x2, Pallas kernels: 45.3 us -> 37.4 us  [count_matrix(): pl.pallas_call(functools.partial(count_kernel, vocab // 4096, unroll), gr...]
    pallas_call x1, Pallas kernels: 29.5 us -> 25.4 us  [compose(): pl.pallas_call(compose_kernel, grid=(n // block,), in_specs=[pl.BlockSpec...]
  transfers between devices with their start and end apart: 7 -> 7, of which waited for: 0 -> 0; matrix products, arithmetic and copies ran while one was open for 3% -> 3% of each run, Pallas kernels for 27% -> 24%
where the time goes in v4:
time: 286 us; the launch traced here: 285 us
  Pallas kernels  253 us (88%)
  local copies, waits for them, and re-layouts  14.3 us (5%)
  other arithmetic  8.91 us (3%)
  starting transfers between devices  6.16 us (2%)
  between operations  3.2 us (1%)
    pallas_call x1, Pallas kernels, layer_one(): pl.pallas_call(layer_one_kernel, grid_spec=pltpu.PrefetchScalarGridSpec(n...  81.5 us
    pallas_call x2, Pallas kernels, count_matrix(): pl.pallas_call(functools.partial(count_kernel, vocab // 4096, unroll), gr...  37.4 us
    pallas_call x1, Pallas kernels, sum_devices(): pl.pallas_call(sum_kernel, in_specs=[vmem] * 5, out_specs=vmem, out_shape...  36 us
    pallas_call x1, Pallas kernels, bottom(): pl.pallas_call(bottom_kernel, grid=(steps + 1,), in_specs=[pl.BlockSpec((...  33.9 us
    pallas_call x1, Pallas kernels, compose(): pl.pallas_call(compose_kernel, grid=(n // block,), in_specs=[pl.BlockSpec...  25.4 us
    pallas_call x1, Pallas kernels, layer_two(): pl.pallas_call(layer_two_kernel, grid=(n // block,), in_specs=[pl.BlockSp...  20.8 us
    pallas_call x1, Pallas kernels, top(): pl.pallas_call(functools.partial(top_kernel, classes), grid=(1,), in_spec...  12.3 us
    sub x1, other arithmetic, adam_update(): params - ADAM_LR * m_hat / (jnp.sqrt(v_hat) + ADAM_EPS)  7.09 us
  transfers between devices with their start and end apart: 7, of which 0 were waited for; matrix products, arithmetic and copies ran while one was open for 3% of the time, Pallas kernels for 24%

profile of v4, /device:TPU:0, one launch (start us, length us, event | category | flops | bytes accessed | tf_op | source)
XLA Modules:
  0.0 285.2 jit_solution(13036333519435647798)
XLA Ops:
  0.6 0.0 copy-start
  0.6 3.4 %collective-permute-start = (bf16[512,768]{1,0:T(8,128)(2,1)}, bf16[512,768]{1,0:T(8,128)(2,1)S(1)}, u32[]{:S(2)}, u32[]{:S(2)}) collective-permute-start(bf16[512,768]{1,0:T(8,128)(2,1)} %refs_0_.1), channel_id=1, source_target_pairs={{0,2},{1,3},{2,0},{3,1},{4,6},{5,7},{6,4},{7,5}} | collective-permute-start | bytes 2359304 | tf_op jit(solution)/shard_map/ppermute | solution.py:621
  4.0 1.5 collective-permute-start.1
  5.5 0.0 collective-permute-start.3
  5.5 3.0 %slice_bitcast_fusion.rows_ref = f32[4108,128]{1,0:T(8,128)} fusion(f32[604313]{0:T(1024)} %param.23), kind=kLoop, calls=%fused_computation.5 | loop fusion | bytes 4206592 | tf_op jit(solution)/shard_map/reshape | solution.py:670
  8.6 0.0 copy-done
  8.6 0.0 copy-start.2
  8.6 1.1 convert.4
  9.7 2.7 weights.1
  12.5 1.0 fusion.3
  13.5 0.0 copy-done.2
  13.5 0.7 fusion.5.front_ref
  14.1 0.0 slice-start
  14.1 0.0 copy-start.3
  14.1 25.4 %compose_ids.1 = (f32[512,256]{1,0:T(8,128)}, f32[512,256]{1,0:T(8,128)}, f32[8192,128]{1,0:T(8,128)}) custom-call(s32[256,128]{1,0:T(8,128)} %fusion.5.front_ref, s32[15,8192]{1,0:T(8,128)} %bitcast.29, s32[15,8192]{1,0:T(8,128)} %bitcast.30), custom_call_target="tpu_custom_call" | custom-call | flops 16106127360 | bytes 10000000 | tf_op jit(solution)/shard_map/compose_ids/pallas_call | solution.py:110
  39.5 0.6 slice.51.self_ids
  40.1 0.4 convert_element_type.13
  40.5 0.4 convert_element_type.14
  40.9 0.7 pad.11.w3s_ref
  41.5 0.7 pad.12.w3n_ref
  42.2 2.6 codes.1
  44.8 0.0 slice-done
  44.8 0.6 pad.13.bias3_ref
  45.4 0.0 copy-done.3
  45.4 0.6 fusion.4
  46.0 0.0 collective-permute-done.refs_2_
  46.0 0.0 copy-start.4
  46.0 0.0 collective-permute-done.1.refs_4_
  46.0 0.5 collective-permute-start.2
  46.6 0.2 collective-permute-start.4
  46.8 0.3 collective-permute-start.5
  47.1 24.2 %count_matrix.2.m_ref = bf16[8192,4096]{1,0:T(8,128)(2,1)} custom-call(f32[512,256]{1,0:T(8,128)} %get-tuple-element.46.low_ref, f32[512,256]{1,0:T(8,128)} %get-tuple-element.47.high_ref), custom_call_target="tpu_custom_call" | custom-call | flops 17179869184 | bytes 67108864 | tf_op jit(solution)/shard_map/count_matrix/pallas_call | solution.py:169
  71.3 0.0 copy-done.4
  71.3 0.0 collective-permute-done.2.refs_6_
  71.3 0.0 copy-start.5
  71.3 0.2 collective-permute-start.6
  71.5 13.2 %count_matrix.3.m_ref = bf16[2048,8192]{1,0:T(8,128)(2,1)} custom-call(f32[128,256]{1,0:T(8,128)} %get-tuple-element.48.low_ref, f32[128,256]{1,0:T(8,128)} %get-tuple-element.49.high_ref), custom_call_target="tpu_custom_call" | custom-call | flops 8589934592 | bytes 33554432 | tf_op jit(solution)/shard_map/count_matrix/pallas_call | solution.py:169
  84.7 0.0 copy-done.5
  84.7 0.0 collective-permute-done.3.refs_1_
  84.7 0.0 collective-permute-done.4.refs_3_
  84.7 0.0 copy-start.6
  84.7 0.0 collective-permute-done.5.refs_5_
  84.8 0.0 copy-start.7
  84.8 0.0 collective-permute-done.6.refs_7_
  84.8 0.8 copy-done.6
  85.6 0.3 copy-done.7
  85.9 81.5 %layer_one.1 = (bf16[8192,768]{1,0:T(8,128)(2,1)}, bf16[8192,768]{1,0:T(8,128)(2,1)}, bf16[8192,256]{1,0:T(8,128)(2,1)}, f32[256,8192]{1,0:T(8,128)}) custom-call(s32[8192]{0:T(1024)} %slice.51.self_ids, bf16[8192,4096]{1,0:T(8,128)(2,1)} %count_matrix.2.m_ref, f32[8192,128]{1,0:T(8,128)} %get-tuple-element.52.codes_ref, bf16[512,768]{1,0:T(8,128)(2,1)} %refs_0_.1, ...), custom_call_target="tpu_custom_call" | custom-call | flops 51539607552 | bytes 67108864 | tf_op jit(solution)/shard_map/layer_one/pallas_call | solution.py:269
  167.4 20.8 %layer_two.1 = (bf16[2048,256]{1,0:T(8,128)(2,1)}, bf16[2048,256]{1,0:T(8,128)(2,1)}, f32[2048,256]{1,0:T(8,128)}) custom-call(bf16[2048,8192]{1,0:T(8,128)(2,1)} %count_matrix.3.m_ref, f32[2048,128]{1,0:T(8,128)} %get-tuple-element.50.codes_ref.codes2_ref, bf16[8192,256]{1,0:T(8,128)(2,1)} %get-tuple-element.58.h_all_ref.h_self_ref.h1_ref, ...), custom_call_target="tpu_custom_call" | custom-call | flops 8589934592 | bytes 33554432 | tf_op jit(solution)/shard_map/layer_two/pallas_call | solution.py:312
  188.2 12.3 %layer_three.1 = (f32[256,256]{1,0:T(8,128)}, f32[256,256]{1,0:T(8,128)}, f32[1032,128]{1,0:T(8,128)}, f32[8,128]{1,0:T(8,128)}, f32[256,2048]{1,0:T(8,128)}, /*index=5*/bf16[256,2048]{1,0:T(8,128)(2,1)}) custom-call(s32[5,512]{1,0:T(8,128)} %bitcast.25, s32[5,512]{1,0:T(8,128)} %bitcast.26, s32[1,512]{1,0:T(1,128)} %bitcast.27, s32[1,512]{1,0:T(1,128)} %bitcast.28, ...), custom_call_target="tpu_custom_call" | custom-call | tf_op jit(solution)/shard_map/layer_three/pallas_call | solution.py:427
  200.5 1.9 reshape_reshape.6.top_ref
  202.4 1.9 reshape_reshape.7.next_ref
  204.4 33.9 %layer_one_back.1.low_ref = f32[3080,128]{1,0:T(8,128)} custom-call(bf16[256,2048]{1,0:T(8,128)(2,1)} %get-tuple-element.64.dagg_ref, bf16[2048,8192]{1,0:T(8,128)(2,1)} %count_matrix.3.m_ref, f32[256,2048]{1,0:T(8,128)} %get-tuple-element.65.dself_ref, f32[256,8192]{1,0:T(8,128)} %get-tuple-element.66.zt_ref, bf16[8192,768]{1,0:T(8,128)(2,1)} %get-tuple-element.67.hs_ref, ...), custom_call_target="tpu_custom_call" | custom-call | flops 8589934592 | bytes 33554432 | tf_op jit(solution)/shard_map/layer_one_back/pallas_call | solution.py:494
  238.3 0.0 copy-start.1
  238.3 36.0 %sum_devices.1 = f32[4736,128]{1,0:T(8,128)} custom-call(f32[3080,128]{1,0:T(8,128)} %layer_one_back.1.low_ref, f32[1032,128]{1,0:T(8,128)} %get-tuple-element.70.mid_ref, f32[306,128]{1,0:T(8,128)} %reshape_reshape.6.top_ref, f32[306,128]{1,0:T(8,128)} %reshape_reshape.7.next_ref, f32[8,128]{1,0:T(8,128)} %get-tuple-element.73.tail_ref), custom_call_target="tpu_custom_call" | custom-call | tf_op jit(solution)/shard_map/sum_devices/pallas_call | solution.py:596
  274.3 1.3 fusion.2
  277.0 0.0 copy-done.1
  277.0 7.1 %divide_subtract_fusion = (f32[604313]{0:T(1024)}, f32[604313]{0:T(1024)}, f32[604313]{0:T(1024)}) fusion(f32[604313]{0:T(1024)S(1)} %copy-done.1, f32[]{:T(128)} %bitcast.13, f32[606208]{0:T(1024)} %bitcast.20, f32[604313]{0:T(1024)} %param.24, f32[604313]{0:T(1024)} %param.25), kind=kLoop, calls=%fused_computation.3 | loop fusion | flops 7856069 | bytes 16920768 | tf_op jit(solution)/shard_map/sub | solution.py:617
  (1 shorter events, 0.0 us)
Async XLA Ops:
  0.6 8.0 %copy-start = (f32[604313]{0:T(1024)S(1)}, f32[604313]{0:T(1024)}, u32[]{:S(2)}) copy-start(f32[604313]{0:T(1024)} %param.23) | copy-start | bytes 7251760
  0.6 45.4 %collective-permute-start = (bf16[512,768]{1,0:T(8,128)(2,1)}, bf16[512,768]{1,0:T(8,128)(2,1)S(1)}, u32[]{:S(2)}, u32[]{:S(2)}) collective-permute-start(bf16[512,768]{1,0:T(8,128)(2,1)} %refs_0_.1), channel_id=1, source_target_pairs={{0,2},{1,3},{2,0},{3,1},{4,6},{5,7},{6,4},{7,5}} | collective-permute-start | bytes 2359304 | tf_op jit(solution)/shard_map/ppermute | solution.py:621
  4.0 42.0 %collective-permute-start.1 = (bf16[512,768]{1,0:T(8,128)(2,1)}, bf16[512,768]{1,0:T(8,128)(2,1)}, u32[]{:S(2)}, u32[]{:S(2)}) collective-permute-start(bf16[512,768]{1,0:T(8,128)(2,1)} %refs_0_.1), channel_id=1, source_target_pairs={{0,4},{1,5},{2,6},{3,7},{4,0},{5,1},{6,2},{7,3}} | collective-permute-start | bytes 2359304 | tf_op jit(solution)/shard_map/ppermute | solution.py:621
  5.5 79.2 %collective-permute-start.3 = (bf16[512,768]{1,0:T(8,128)(2,1)}, bf16[512,768]{1,0:T(8,128)(2,1)}, u32[]{:S(2)}, u32[]{:S(2)}) collective-permute-start(bf16[512,768]{1,0:T(8,128)(2,1)} %refs_0_.1), channel_id=1, source_target_pairs={{0,1},{1,0},{2,3},{3,2},{4,5},{5,4},{6,7},{7,6}} | collective-permute-start | bytes 2359304 | tf_op jit(solution)/shard_map/ppermute | solution.py:621
  8.6 4.9 %copy-start.2 = (s32[32768]{0:T(1024)S(1)}, s32[32768]{0:T(1024)}, u32[]{:S(2)}) copy-start(s32[32768]{0:T(1024)} %param.14) | copy-start | bytes 393220
  14.1 30.7 %slice-start = ((f32[604313]{0:T(1024)}), f32[153]{0:T(256)S(1)}, s32[]{:S(2)}) async-start(f32[604313]{0:T(1024)} %param.23), calls=%async_computation | async-start | bytes 2048 | tf_op jit(solution)/shard_map/slice | solution.py:675
  14.1 31.3 %copy-start.3 = (f32[16,256]{1,0:T(8,128)S(1)}, f32[16,256]{1,0:T(8,128)}, u32[]{:S(2)}) copy-start(f32[16,256]{1,0:T(8,128)} %get-tuple-element.57) | copy-start | bytes 49156
  46.0 25.3 %copy-start.4 = (bf16[512,768]{1,0:T(8,128)(2,1)}, bf16[512,768]{1,0:T(8,128)(2,1)S(1)}, u32[]{:S(2)}) copy-start(bf16[512,768]{1,0:T(8,128)(2,1)S(1)} %collective-permute-done.refs_2_) | copy-start | bytes 2359300
  46.0 25.2 %collective-permute-start.2 = (bf16[512,768]{1,0:T(8,128)(2,1)S(1)}, bf16[512,768]{1,0:T(8,128)(2,1)S(1)}, u32[]{:S(2)}, u32[]{:S(2)}) collective-permute-start(bf16[512,768]{1,0:T(8,128)(2,1)S(1)} %collective-permute-done.refs_2_), channel_id=1, source_target_pairs={{0,4},{1,5},{2,6},{3,7},{4,0},{5,1},{6,2},{7,3}} | collective-permute-start | bytes 2359304 | tf_op jit(solution)/shard_map/ppermute | solution.py:621
  46.6 38.2 %collective-permute-start.4 = (bf16[512,768]{1,0:T(8,128)(2,1)S(1)}, bf16[512,768]{1,0:T(8,128)(2,1)S(1)}, u32[]{:S(2)}, u32[]{:S(2)}) collective-permute-start(bf16[512,768]{1,0:T(8,128)(2,1)S(1)} %collective-permute-done.refs_2_), channel_id=1, source_target_pairs={{0,1},{1,0},{2,3},{3,2},{4,5},{5,4},{6,7},{7,6}} | collective-permute-start | bytes 2359304 | tf_op jit(solution)/shard_map/ppermute | solution.py:621
  46.8 38.0 %collective-permute-start.5 = (bf16[512,768]{1,0:T(8,128)(2,1)}, bf16[512,768]{1,0:T(8,128)(2,1)S(1)}, u32[]{:S(2)}, u32[]{:S(2)}) collective-permute-start(bf16[512,768]{1,0:T(8,128)(2,1)} %collective-permute-done.1.refs_4_), channel_id=1, source_target_pairs={{0,1},{1,0},{2,3},{3,2},{4,5},{5,4},{6,7},{7,6}} | collective-permute-start | bytes 2359304 | tf_op jit(solution)/shard_map/ppermute | solution.py:621
  71.3 13.4 %copy-start.5 = (bf16[512,768]{1,0:T(8,128)(2,1)}, bf16[512,768]{1,0:T(8,128)(2,1)S(1)}, u32[]{:S(2)}) copy-start(bf16[512,768]{1,0:T(8,128)(2,1)S(1)} %collective-permute-done.2.refs_6_) | copy-start | bytes 2359300
  71.3 13.5 %collective-permute-start.6 = (bf16[512,768]{1,0:T(8,128)(2,1)S(1)}, bf16[512,768]{1,0:T(8,128)(2,1)}, u32[]{:S(2)}, u32[]{:S(2)}) collective-permute-start(bf16[512,768]{1,0:T(8,128)(2,1)S(1)} %collective-permute-done.2.refs_6_), channel_id=1, source_target_pairs={{0,1},{1,0},{2,3},{3,2},{4,5},{5,4},{6,7},{7,6}} | collective-permute-start | bytes 2359304 | tf_op jit(solution)/shard_map/ppermute | solution.py:621
  84.7 0.9 copy-start.6
  84.8 1.1 copy-start.7
  238.3 38.7 %copy-start.1 = (f32[604313]{0:T(1024)S(1)}, f32[604313]{0:T(1024)}, u32[]{:S(2)}) copy-start(f32[604313]{0:T(1024)} %param.23) | copy-start | bytes 7251760
